TPU v7x, 32 devices: a whole 2x2x4 slice. The times are simulated.
32 devices in a mesh: dp: 8 (over y, x, core), mp: 4 (over z).
Axes of the slice: x: 2, y: 2, z: 4, core: 2. Of those that a mesh axis runs over, the one named last changes fastest.
Arguments:
- hidden_in: float32 [16384, 768], P(('dp', 'mp')), may hold values from -6 to 6
- first_values: bfloat16 [16384, 384], P('dp', 'mp'), may hold values from -6 to 6
- first_length: int32 [8], P('dp'), may hold values from 1024 to 2048, as said below
- pre_gain: float32 [768], replicated, may hold values from 0.25 to 1.75
- pre_shift: float32 [768], replicated, may hold values from -1.75 to 1.75
- w_query: bfloat16 [768, 768], P(None, 'mp'), may hold values from -0.21875 to 0.21875
- b_query: float32 [768], P('mp'), may hold values from -3 to 3
- w_key: bfloat16 [768, 768], P(None, 'mp'), may hold values from -0.21875 to 0.21875
- w_value: bfloat16 [768, 384], P(None, 'mp'), may hold values from -0.21875 to 0.21875
- b_value: float32 [384], P('mp'), may hold values from -3 to 3
- w_out: bfloat16 [768, 768], P('mp'), may hold values from -1.75 to 1.75
- b_out: float32 [768], replicated, may hold values from -3 to 3
- mid_gain: float32 [768], replicated, may hold values from 0.25 to 1.75
- mid_shift: float32 [768], replicated, may hold values from -1.75 to 1.75
- w_up: bfloat16 [768, 3072], P(None, 'mp'), may hold values from -0.21875 to 0.21875
- b_up: float32 [3072], P('mp'), may hold values from -3 to 3
- w_down: bfloat16 [3072, 768], P('mp'), may hold values from -0.109375 to 0.109375
- b_down: float32 [768], replicated, may hold values from -3 to 3
- grad_out: float32 [16384, 768], P(('dp', 'mp')), may hold values from -6 to 6
Outputs:
- layer_out: float32 [16384, 768], P(('dp', 'mp'))
- grad_in: float32 [16384, 768], P(('dp', 'mp'))
- grad_first_values: float32 [16384, 384], P('dp', 'mp')
- grad_pre_gain: float32 [768], replicated
- grad_pre_shift: float32 [768], replicated
- grad_w_query: float32 [768, 768], P(None, 'mp')
- grad_b_query: float32 [768], P('mp')
- grad_w_key: float32 [768, 768], P(None, 'mp')
- grad_w_value: float32 [768, 384], P(None, 'mp')
- grad_b_value: float32 [384], P('mp')
- grad_w_out: float32 [768, 768], P('mp')
- grad_b_out: float32 [768], replicated
- grad_mid_gain: float32 [768], replicated
- grad_mid_shift: float32 [768], replicated
- grad_w_up: float32 [768, 3072], P(None, 'mp')
- grad_b_up: float32 [3072], P('mp')
- grad_w_down: float32 [3072, 768], P('mp')
- grad_b_down: float32 [768], replicated
Inputs may be any that keep to these rules, and one draw needn't show every extreme that they name: `first_length`: each entry is 2048 / 2 (two documents in the block) or 2048 (one document); half of the entries take each value.
All inputs are finite; a program needn't handle non-finite values.
Results may differ from a plain program's by a relative error of at most 0.02.
Values may be sent and summed in bfloat16 or wider, within the bound.
A program may use at most 192 MiB of HBM per device.

v0:
```python
import functools

import jax
import jax.numpy as jnp
from jax import lax
from jax.experimental import pallas as pl
from jax.experimental.pallas import tpu as pltpu
from jax.sharding import PartitionSpec as P

HEAD_DIM = 64
EPSILON = 1e-05
NEG_LARGE = -1e30
MESH = pl.DeviceIdType.MESH
BF = jnp.bfloat16
F32 = jnp.float32
ANY = pl.BlockSpec(memory_space=pl.ANY)
VM = pl.BlockSpec(memory_space=pltpu.VMEM)
SM = pl.BlockSpec(memory_space=pltpu.SMEM)
VMEM_LIMIT = 60 << 20
LANE = 128
PLANE = 8
RING = 4
HEADS_AT = ((0, 1, 6), (2, 7, 8), (3, 9, 10), (4, 5, 11))
FRESH = ((0, 0, 96, 0, 0), (1, 0, 32, 0, 96), (1, 32, 64, 1, 0), (2, 0, 64, 2, 0), (2, 64, 32, 3, 0), (3, 0, 96, 3, 32))
KEPT = ((0, 0, 64, 128), (1, 0, 96, 96), (2, 0, 96, 64), (3, 32, 64, 128))
MOVED = ((0, 64, 32, 1, 64), (3, 0, 32, 2, 160))


def dot(left, right, left_dim, right_dim):
    return lax.dot_general(
        left, right, (((left_dim,), (right_dim,)), ((), ())), preferred_element_type=F32
    )


def layer_norm(values, gain, shift):
    center = values - jnp.mean(values, -1, keepdims=True)
    spread = jnp.mean(center * center, -1, keepdims=True)
    return center * lax.rsqrt(spread + EPSILON) * gain + shift


def gelu_tanh(values):
    return (
        0.5
        * values
        * (1.0 + jnp.tanh(0.7978845608028654 * (values + 0.044715 * values * values * values)))
    )


def lanes(start, size):
    return pl.ds(pl.multiple_of(start, LANE), size)


def rows_of(start, size, unit):
    return pl.ds(pl.multiple_of(start, unit), size)


class Place:
    def __init__(self, ring, planes=1):
        self.ring = ring
        self.planes = planes
        self.d = lax.axis_index("dp")
        self.m = lax.axis_index("mp")
        d = self.d
        self.core = lax.rem(d, 2)
        self.x = lax.rem(d // 2, 2)
        self.y = lax.rem(d // 4, 2)
        self.to_core = (d + 1 - 2 * self.core, self.m)
        self.to_x = (d + 2 - 4 * self.x, self.m)
        self.to_y = (d + 4 - 8 * self.y, self.m)
        self.pair = self.m + 1 - 2 * lax.rem(self.m, 2)
        self.across = lax.rem(self.m + 2, RING)
        self.corner = RING - 1 - self.m

    def z(self, shift):
        return lax.rem(self.m + shift, self.ring)

    def to_z(self, shift):
        return (self.d, self.z(shift))

    def shift_to(self, position):
        return lax.rem(position - self.m + self.ring, self.ring)

    def head(self, slot):
        value = HEADS_AT[RING - 1][slot]
        for k in range(RING - 1):
            value = jnp.where(self.m == k, HEADS_AT[k][slot], value)
        return value

    def steps(self):
        return [PLANE << b for b in range(self.planes.bit_length() - 1)]

    def to_plane(self, step):
        return (self.d + step - 2 * step * lax.rem(self.d // step, 2), self.m)

    def barrier(self):
        sem = pltpu.get_barrier_semaphore()
        peers = [self.to_z(j) for j in range(1, self.ring)]
        peers += [self.to_core, self.to_x, self.to_y]
        peers += [self.to_plane(step) for step in self.steps()]
        for peer in peers:
            pl.semaphore_signal(sem, inc=1, device_id=peer, device_id_type=MESH)
        pl.semaphore_wait(sem, len(peers))

    def slot(self, x_first):
        if x_first:
            return self.core * 4 + self.y * 2 + self.x
        return self.core * 4 + self.x * 2 + self.y


def remote(src, dst, send, recv, device):
    return pltpu.make_async_remote_copy(
        src_ref=src,
        dst_ref=dst,
        send_sem=send,
        recv_sem=recv,
        device_id=device,
        device_id_type=MESH,
    )


class Gather:
    def __init__(self, place, src, dst, send, recv, item, first_row, rows, x_first):
        self.place, self.src, self.dst = place, src, dst
        self.send, self.recv, self.item = send, recv, item
        self.first_row, self.part, self.x_first = first_row, rows // PLANE, x_first

    def window(self, start, size):
        part = self.part
        return rows_of(self.first_row + start * part, size * part, part & -part)

    def copy(self, stage, k):
        place = self.place
        slot = place.slot(self.x_first)
        near, far = (place.to_x, place.to_y) if self.x_first else (place.to_y, place.to_x)
        shard = (place.across, place.pair, place.corner)[k]
        window = self.window(slot, 1)
        if stage == 0:
            shard, target = place.m, (place.d, place.across)
        elif stage == 1:
            shard, target = (place.m, place.across)[k], (place.d, place.pair)
        elif stage == 2:
            target = near
        elif stage == 3:
            window, target = self.window((slot // 2) * 2, 2), far
        else:
            window, target = self.window(place.core * 4, 4), place.to_core
        own = stage == 0 or (stage == 1 and k == 0)
        source = self.src.at[window] if own else self.dst.at[shard, window]
        return remote(
            source,
            self.dst.at[shard, window],
            self.send.at[self.item, stage, k],
            self.recv.at[self.item, stage, k],
            target,
        )

    def start(self, stage):
        if stage == 0:
            self.copy(0, 0).start()
            self.copy(1, 0).start()
        elif stage == 1:
            self.copy(0, 0).wait_recv()
            self.copy(1, 1).start()
        else:
            for k in range(2 if stage == 2 else 3):
                self.copy(stage - 1, k).wait_recv()
            for k in range(3):
                self.copy(stage, k).start()

    def arrive(self):
        for k in range(3):
            self.copy(4, k).wait_recv()

    def drain(self):
        for stage, copies in enumerate((1, 2, 3, 3, 3)):
            for k in range(copies):
                self.copy(stage, k).wait_send()


class Reduce:
    def __init__(self, place, src, bufs, out, send, recv, item, x_first):
        self.place, self.src, self.out = place, src, out
        self.r_core, self.r_far, self.r_near, self.r_z, self.r_plane = bufs
        self.send, self.recv, self.item, self.x_first = send, recv, item, x_first
        self.part = out.shape[0] // PLANE
        if x_first:
            self.near, self.far = place.to_x, place.to_y
            self.near_bit, self.far_bit = place.x, place.y
        else:
            self.near, self.far = place.to_y, place.to_x
            self.near_bit, self.far_bit = place.y, place.x

    def rows(self, start, size):
        return rows_of(start * self.part, size * self.part, self.part & -self.part)

    def copy(self, stage, k):
        place = self.place
        if stage == 0:
            src = self.src.at[k, self.rows((1 - place.core) * 4, 4)]
            dst, target = self.r_core.at[k], place.to_core
        elif stage == 1:
            src = self.r_core.at[k, self.rows((1 - self.far_bit) * 2, 2)]
            dst, target = self.r_far.at[k], self.far
        elif stage == 2:
            src = self.r_far.at[k, self.rows(1 - self.near_bit, 1)]
            dst, target = self.r_near.at[k], self.near
        elif stage == 3:
            src = self.r_near.at[(place.pair, place.corner)[k]]
            dst, target = self.r_z.at[k], (place.d, place.pair)
        elif stage == 4:
            src = self.r_near.at[place.across]
            dst, target = self.r_z.at[2], (place.d, place.across)
        else:
            slot = place.slot(self.x_first)
            if stage == 5:
                window, target = self.rows(slot, 1), self.near
            elif stage == 6:
                window, target = self.rows((slot // 2) * 2, 2), self.far
            else:
                window, target = self.rows(place.core * 4, 4), place.to_core
            src = dst = self.out.at[window]
        return remote(
            src, dst, self.send.at[self.item, stage, k], self.recv.at[self.item, stage, k], target
        )

    def members(self, stage):
        return range((RING, RING, RING, 2, 1, 1, 1, 1)[stage])

    def start(self, stage):
        for k in self.members(stage):
            self.copy(stage, k).start()

    def wait(self, stage):
        for k in self.members(stage):
            self.copy(stage, k).wait_recv()

    def fold_one(self, stage, k):
        place, part = self.place, self.part
        if stage == 0:
            kept, base, into, size = self.src, place.core * 4 * part, self.r_core, 4 * part
        elif stage == 1:
            kept, base, into, size = self.r_core, self.far_bit * 2 * part, self.r_far, 2 * part
        else:
            kept, base, into, size = self.r_far, self.near_bit * part, self.r_near, part
        unit = part & -part
        step = min(part, 32)
        self.copy(stage, k).wait_recv()

        def add(i, carry):
            mine = kept[k, rows_of(base + i * step, step, min(unit, step)), :].astype(F32)
            here = rows_of(i * step, step, step)
            into[k, here, :] = (into[k, here, :].astype(F32) + mine).astype(BF)
            return carry

        lax.fori_loop(0, size // step, add, 0)
        if stage < 2:
            self.copy(stage + 1, k).start()

    def fold(self, stage):
        for k in self.members(stage):
            self.fold_one(stage, k)
        if stage == 2:
            self.start(3)

    def fold_pair(self):
        place = self.place
        self.wait(3)
        other = self.r_near[place.across].astype(F32) + self.r_z[1].astype(F32)
        self.r_near[place.across] = other.astype(BF)
        self.start(4)
        mine = self.r_near[place.m].astype(F32) + self.r_z[0].astype(F32)
        self.r_near[place.m] = mine.astype(BF)

    def finish_sum(self):
        place = self.place
        self.wait(4)
        here = self.rows(place.slot(self.x_first), 1)
        value = self.r_near[place.m].astype(F32) + self.r_z[2].astype(F32)
        self.out[here, :] = value.astype(BF)
        for b, step in enumerate(place.steps()):
            copy = remote(
                self.out.at[here],
                self.r_plane.at[b],
                self.send.at[self.item, 8 + b, 0],
                self.recv.at[self.item, 8 + b, 0],
                place.to_plane(step),
            )
            copy.start()
            copy.wait()
            mine = self.out[here, :].astype(F32)
            self.out[here, :] = (mine + self.r_plane[b].astype(F32)).astype(BF)
        self.start(5)

    def spread(self, stage):
        self.wait(stage - 1)
        self.start(stage)

    def drain(self, first):
        for stage in range(first, 8):
            for k in self.members(stage):
                self.copy(stage, k).wait_send()

    @staticmethod
    def buffers(rows, width, planes):
        part = rows // PLANE
        extra = max(planes.bit_length() - 1, 1)
        return [
            pltpu.VMEM((RING, 4 * part, width), BF),
            pltpu.VMEM((RING, 2 * part, width), BF),
            pltpu.VMEM((RING, part, width), BF),
            pltpu.VMEM((3, part, width), BF),
            pltpu.VMEM((extra, part, width), BF),
        ]


def diagonal_mask(scores, key_start, query_start):
    keys = lax.broadcasted_iota(jnp.int32, scores.shape, 0) + key_start
    queries = lax.broadcasted_iota(jnp.int32, scores.shape, 1) + query_start
    return keys <= queries


def other_document(boundary, key_start, query_start):
    crossing = jnp.logical_and(boundary > key_start, boundary <= query_start)
    return jnp.where(crossing, NEG_LARGE, 0.0)


def forward_kernel(
    ring,
    heads_here,
    length_ref,
    hidden_ref,
    gain_ref,
    shift_ref,
    wt_ref,
    bias_ref,
    first_ref,
    wo_ref,
    wu_ref,
    wd_ref,
    context_ref,
    normed_ref,
    qk_ref,
    v_ref,
    lse_ref,
    exact_ref,
    wt_all,
    bias_all,
    wo_far,
    wu_far,
    wd_far,
    y_send,
    vy_send,
    c_send,
    keys,
    gsend,
    grecv,
    bsend,
    brecv,
    qsend,
    qrecv,
    vsend,
    vrecv,
    fsend,
    frecv,
    csend,
    crecv,
):
    place = Place(ring)
    m = place.m
    count = hidden_ref.shape[0]
    total = ring * count
    piece = first_ref.shape[0]
    half = total // 2
    hd = HEAD_DIM
    pack_rows = wt_ref.shape[0]
    place.barrier()
    half_pack = pack_rows // 2
    small = [
        Gather(place, wt_ref, wt_all, gsend, grecv, i, i * half_pack, half_pack, i == 0)
        for i in range(2)
    ]
    big = [
        Gather(place, wo_ref, wo_far, gsend, grecv, 2, 0, wo_ref.shape[0], True),
        Gather(place, wu_ref, wu_far, gsend, grecv, 3, 0, wu_ref.shape[0], True),
        Gather(place, wd_ref, wd_far, gsend, grecv, 4, 0, wd_ref.shape[0], False),
    ]
    for item in small:
        item.start(0)

    def bias_copy(j):
        return remote(
            bias_ref, bias_all.at[m], bsend.at[j - 1], brecv.at[j - 1], place.to_z(j)
        )

    for j in range(1, ring):
        bias_copy(j).start()

    def moved_copy(i):
        _, row, rows, to, row_there = MOVED[i]
        return remote(
            first_ref.at[pl.ds(row, rows)],
            v_ref.at[pl.ds(row_there, rows)],
            fsend.at[0],
            frecv.at[0],
            (place.d, to),
        )

    for i, move in enumerate(MOVED):

        @pl.when(m == move[0])
        def _(i=i):
            moved_copy(i).start()

    for at, row, rows, row_there in KEPT:

        @pl.when(m == at)
        def _(row=row, rows=rows, row_there=row_there):
            v_ref[row_there : row_there + rows, :] = first_ref[row : row + rows, :]

    for item in big:
        item.start(0)

    normed_ref[...] = layer_norm(hidden_ref[...], gain_ref[...], shift_ref[...]).astype(BF)
    wt_all[m] = wt_ref[...]
    bias_all[m] = bias_ref[...]

    for stage in (1, 2):
        for item in small:
            item.start(stage)
    for item in big:
        item.start(1)
    for stage in (3, 4):
        for item in small:
            item.start(stage)
    for j in range(1, ring):
        bias_copy(j).wait_recv()
    for item in small:
        item.arrive()

    own = lanes(m * count, count)

    def qk_copy(slot, to):
        return remote(
            y_send.at[to, slot],
            qk_ref.at[slot, :, own],
            qsend.at[to, slot],
            qrecv.at[slot, place.shift_to(to) - 1],
            (place.d, to),
        )

    def v_copy(i):
        shard, row, rows, to, row_there = FRESH[i]
        return remote(
            vy_send.at[shard, pl.ds(row, rows)],
            v_ref.at[pl.ds(row_there, rows), own],
            vsend.at[i],
            vrecv.at[i, place.shift_to(to) - 1],
            (place.d, to),
        )

    where_is = {head: (to, slot) for to, heads in enumerate(HEADS_AT) for slot, head in enumerate(heads)}
    v_row = 2 * hd * heads_here

    for shard in range(ring):
        out = dot(wt_all[shard], normed_ref[...], 1, 1)
        out = out + jnp.transpose(bias_all[shard, :, 0:pack_rows])[:, 0:1]
        for i in range(heads_here):
            to, slot = where_is[heads_here * shard + i]
            row = 2 * hd * i
            y_send[to, slot, 0:hd, :] = (out[row : row + hd] * (hd**-0.5)).astype(BF)
            y_send[to, slot, hd : 2 * hd, :] = out[row + hd : row + 2 * hd].astype(BF)
        vy_send[shard] = out[v_row : v_row + piece].astype(BF)

    def share(slot):
        for to in range(ring):

            @pl.when(m == to)
            def _(to=to):
                qk_ref[slot, :, own] = y_send[to, slot]

            @pl.when(m != to)
            def _(to=to):
                qk_copy(slot, to).start()

    share(0)
    for i, (shard, row, rows, to, row_there) in enumerate(FRESH):

        @pl.when(m == to)
        def _(shard=shard, row=row, rows=rows, row_there=row_there):
            v_ref[row_there : row_there + rows, own] = vy_send[shard, row : row + rows, :]

        @pl.when(m != to)
        def _(i=i):
            v_copy(i).start()

    for slot in range(1, heads_here):
        share(slot)

    def qk_arrive(slot):
        for shift in range(1, ring):
            remote(
                y_send.at[0, slot],
                qk_ref.at[slot, :, own],
                qsend.at[0, slot],
                qrecv.at[slot, shift - 1],
                place.to_z(shift),
            ).wait_recv()

    qk_arrive(0)
    for i, (shard, row, rows, to, row_there) in enumerate(FRESH):

        @pl.when(m == to)
        def _(i=i, shard=shard, row=row, rows=rows, row_there=row_there):
            for shift in range(1, ring):
                remote(
                    vy_send.at[shard, pl.ds(row, rows)],
                    v_ref.at[pl.ds(row_there, rows), own],
                    vsend.at[i],
                    vrecv.at[i, shift - 1],
                    place.to_z(shift),
                ).wait_recv()

    for i, move in enumerate(MOVED):

        @pl.when(m == move[3])
        def _(i=i):
            moved_copy(i).wait_recv()

    boundary = length_ref[0]
    block = count

    def context_copy(h, j):
        return remote(
            c_send.at[pl.ds(hd * h, hd), lanes(place.z(j) * count, count)],
            context_ref.at[rows_of(place.head(h) * hd, hd, hd)],
            csend.at[h, j - 1],
            crecv.at[h, j - 1],
            place.to_z(j),
        )

    for h in range(heads_here):
        if h > 0:
            qk_arrive(h)
        keys[...] = jnp.transpose(qk_ref[h, hd : 2 * hd, :])
        for qi in range(ring):
            query_start = qi * block
            q = qk_ref[h, 0:hd, query_start : query_start + block]
            top = None
            for ki in range(qi + 1):
                key_start = ki * block
                v = v_ref[hd * h : hd * h + hd, key_start : key_start + block]
                scores = dot(keys[key_start : key_start + block, :], q, 1, 0)
                if ki == qi:
                    scores = jnp.where(
                        diagonal_mask(scores, key_start, query_start), scores, NEG_LARGE
                    )
                elif key_start < half <= query_start:
                    scores = scores + other_document(boundary, key_start, query_start)
                block_top = jnp.max(scores, 0, keepdims=True)
                new_top = block_top if top is None else jnp.maximum(top, block_top)
                p = jnp.exp(scores - new_top)
                p_sum = jnp.sum(p, 0, keepdims=True)
                part = dot(v, p.astype(BF), 1, 0)
                if top is None:
                    run_sum, running = p_sum, part
                else:
                    factor = jnp.exp(top - new_top)
                    run_sum = run_sum * factor + p_sum
                    running = running * factor + part
                top = new_top
            result = running / run_sum
            exact_ref[hd * h : hd * h + hd, query_start : query_start + block] = result
            c_send[hd * h : hd * h + hd, query_start : query_start + block] = result.astype(BF)
            lse_ref[h, :, query_start : query_start + block] = top + jnp.log(run_sum)
        for j in range(1, ring):
            context_copy(h, j).start()
        context_ref[rows_of(place.head(h) * hd, hd, hd), :] = c_send[hd * h : hd * h + hd, own]
        for item in big:
            item.start(2 + h)

    for item in big:
        item.arrive()
    for h in range(heads_here):
        for j in range(1, ring):
            context_copy(h, j).wait_recv()
    for item in small + big:
        item.drain()
    for j in range(1, ring):
        bias_copy(j).wait_send()
        for h in range(heads_here):
            context_copy(h, j).wait_send()
    for to in range(ring):

        @pl.when(m != to)
        def _(to=to):
            for slot in range(heads_here):
                qk_copy(slot, to).wait_send()

    for i, (shard, row, rows, to, row_there) in enumerate(FRESH):

        @pl.when(m != to)
        def _(i=i):
            v_copy(i).wait_send()

    for i, move in enumerate(MOVED):

        @pl.when(m == move[0])
        def _(i=i):
            moved_copy(i).wait_send()


def forward_call(ring, heads_here, length, hidden, gain, shift, wt, bias, first_t, wo, wu, wd):
    count, width = hidden.shape
    total = ring * count
    hd = HEAD_DIM
    piece = first_t.shape[0]
    others = ring - 1
    sds = jax.ShapeDtypeStruct
    dma = pltpu.SemaphoreType.DMA
    return pl.pallas_call(
        functools.partial(forward_kernel, ring, heads_here),
        out_shape=(
            sds((ring * heads_here * hd, count), BF),
            sds((count, width), BF),
            sds((heads_here, 2 * hd, total), BF),
            sds((heads_here * hd, total), BF),
            sds((heads_here, 1, total), F32),
            sds((heads_here * hd, total), F32),
            sds((ring,) + wt.shape, BF),
            sds((ring,) + bias.shape, F32),
            sds((ring,) + wo.shape, BF),
            sds((ring,) + wu.shape, BF),
            sds((ring,) + wd.shape, BF),
        ),
        in_specs=[SM] + [VM] * 6 + [ANY] * 3,
        out_specs=[VM] * 8 + [ANY] * 3,
        scratch_shapes=[
            pltpu.VMEM((ring, heads_here, 2 * hd, count), BF),
            pltpu.VMEM((ring, piece, count), BF),
            pltpu.VMEM((heads_here * hd, total), BF),
            pltpu.VMEM((total, hd), BF),
            dma((5, 5, 3)),
            dma((5, 5, 3)),
            dma((others,)),
            dma((others,)),
            dma((ring, heads_here)),
            dma((heads_here, others)),
            dma((len(FRESH),)),
            dma((len(FRESH), others)),
            dma((1,)),
            dma((1,)),
            dma((heads_here, others)),
            dma((heads_here, others)),
        ],
        compiler_params=pltpu.CompilerParams(
            collective_id=0, has_side_effects=True, vmem_limit_bytes=VMEM_LIMIT
        ),
        name="forward",
    )(length, hidden, gain, shift, wt, bias, first_t, wo, wu, wd)


def backward_kernel(
    ring,
    heads_here,
    planes,
    length_ref,
    context_ref,
    hidden_ref,
    grad_out_ref,
    pre_gain_ref,
    rows_ref,
    bias_ref,
    qk_hbm,
    v_hbm,
    lse_hbm,
    exact_hbm,
    normed_hbm,
    wt_hbm,
    wo_hbm,
    wo_far_hbm,
    wu_hbm,
    wu_far_hbm,
    wd_hbm,
    wd_far_hbm,
    layer_ref,
    grad_in_ref,
    first_ref,
    pack_sum,
    wo_sum,
    wu_sum,
    wd_sum,
    vector_sum,
    qk_ref,
    v_ref,
    lse_ref,
    exact_ref,
    normed_ref,
    wt_all,
    wo_all,
    wu_all,
    wd_all,
    middle_ref,
    mid_ref,
    mid_t,
    down_ref,
    down_t,
    act_ref,
    gup_ref,
    wo_share,
    g_all,
    keys,
    vals,
    delta,
    dq,
    dqk_send,
    dv_send,
    grad_ref,
    vector_held,
    vector_came,
    lsem,
    gsend,
    grecv,
    qsend,
    qrecv,
    vsend,
    vrecv,
    fsend,
    frecv,
    rsend,
    rrecv,
    wsend,
    wrecv,
    *bufs,
):
    place = Place(ring, planes)
    m = place.m
    count, width = hidden_ref.shape
    total = ring * count
    half = total // 2
    hd = HEAD_DIM
    piece = first_ref.shape[0]
    out_rows = wo_hbm.shape[0]
    pack_lanes = grad_ref.shape[1]
    tile = count // 4
    own = lanes(m * count, count)

    def shard_of(j):
        return lax.rem(m - j + ring, ring)

    loads = {}

    def load(name, src, dst):
        loads[name] = pltpu.make_async_copy(src, dst, lsem.at[len(loads)])
        loads[name].start()

    for j in range(ring):
        into = wo_all.at[rows_of(shard_of(j) * out_rows, out_rows, 16)]
        load(("wo", j), wo_hbm if j == 0 else wo_far_hbm.at[shard_of(j)], into)
    for j in range(ring):
        s = shard_of(j)
        load(("wu", j), wu_hbm if j == 0 else wu_far_hbm.at[s], wu_all.at[s])
        load(("wd", j), wd_hbm if j == 0 else wd_far_hbm.at[s], wd_all.at[s])
    load("v", v_hbm, v_ref)
    load("qk", qk_hbm, qk_ref)
    load("lse", lse_hbm, lse_ref)
    load("exact", exact_hbm, exact_ref)
    load("normed", normed_hbm, normed_ref)
    load("wt", wt_hbm, wt_all)
    place.barrier()

    def row(i):
        return rows_ref[i : i + 1, :]

    b_out, mid_gain, mid_shift, b_down = row(0), row(1), row(2), row(3)
    act_ref[...] = jnp.transpose(context_ref[...])
    vector_held[0] = jnp.zeros_like(vector_held[0])
    wo_share[:, out_rows:, :] = jnp.zeros_like(wo_share[:, out_rows:, :])
    grad_ref[:, 2 * hd * heads_here + piece :, :] = jnp.zeros_like(
        grad_ref[:, 2 * hd * heads_here + piece :, :]
    )
    for j in range(ring):
        loads[("wo", j)].wait()

    def project(i, carry):
        here = rows_of(i * tile, tile, tile)
        attended = dot(act_ref[here, :], wo_all[...], 1, 0) + b_out
        middle = hidden_ref[here, :] + attended
        middle_ref[here, :] = middle
        layer_ref[here, :] = middle + b_down
        mid_ref[here, :] = layer_norm(middle, mid_gain, mid_shift).astype(BF)
        grad_down = grad_out_ref[here, :].astype(BF)
        down_ref[here, :] = grad_down
        grad_in_ref[here, :] = jnp.zeros((tile, width), F32)
        return carry + jnp.sum(grad_down.astype(F32), 0, keepdims=True)

    zero_row = jnp.zeros((1, width), F32)
    grad_b_down = lax.fori_loop(0, count // tile, project, zero_row)
    mid_t[...] = jnp.transpose(mid_ref[...])
    down_t[...] = jnp.transpose(down_ref[...])

    down = Reduce(place, wd_all, bufs[0:5], wd_sum, rsend, rrecv, 0, False)
    up = Reduce(place, wu_all, bufs[5:10], wu_sum, rsend, rrecv, 1, True)
    out = Reduce(place, wo_share, bufs[10:15], wo_sum, rsend, rrecv, 2, True)
    pack = Reduce(
        place, wu_all.at[:, pl.ds(0, pack_lanes)], bufs[15:20], pack_sum, rsend, rrecv, 3, True
    )

    big = count // 2
    for j in range(ring):
        loads[("wu", j)].wait()
        loads[("wd", j)].wait()
        s = shard_of(j)
        b_up = bias_ref[s, 0:1, pack_lanes:]

        def feed(i, carry, j=s, b_up=b_up):
            here = rows_of(i * big, big, big)
            u = dot(mid_ref[here, :], wu_all[j], 1, 0) + b_up
            grad_act = dot(down_ref[here, :], wd_all[j], 1, 1)
            square = u * u
            t = jnp.tanh(0.7978845608028654 * (u + 0.044715 * u * square))
            act = (0.5 * u * (1.0 + t)).astype(BF)
            slope = 0.5 * (1.0 + t) + (0.5 * 0.7978845608028654) * u * (1.0 - t * t) * (
                1.0 + 0.134145 * square
            )
            grad_up = (grad_act * slope).astype(BF)
            act_ref[here, :] = act
            gup_ref[here, :] = grad_up
            layer_ref[here, :] += dot(act, wd_all[j], 1, 0)
            grad_in_ref[here, :] += dot(grad_up, wu_all[j], 1, 1)
            return carry + jnp.sum(grad_up.astype(F32), 0, keepdims=True)

        grad_b_up = lax.fori_loop(0, count // big, feed, jnp.zeros((1, wu_all.shape[2]), F32))
        vector_held[0, pl.ds(s, 1), pack_lanes:] = grad_b_up

        def weigh(i, carry, j=s):
            here = lanes(i * 256, 256)
            wu_all[j, :, here] = dot(mid_t[...], gup_ref[:, here], 1, 0).astype(BF)
            wd_all[j, :, here] = dot(down_t[...], act_ref[:, here], 1, 0).astype(BF)
            return carry

        lax.fori_loop(0, wu_all.shape[2] // 256, weigh, 0)
        down.copy(0, s).start()
        up.copy(0, s).start()
        if j > 0:
            down.fold_one(0, shard_of(j - 1))
            up.fold_one(0, shard_of(j - 1))

    def middle_back(i, carry):
        here = rows_of(i * tile, tile, tile)
        middle = middle_ref[here, :]
        center = middle - jnp.mean(middle, -1, keepdims=True)
        scale = lax.rsqrt(jnp.mean(center * center, -1, keepdims=True) + EPSILON)
        unit = center * scale
        grad = grad_in_ref[here, :]
        grad_unit = grad * mid_gain
        grad_middle = grad_out_ref[here, :] + scale * (
            grad_unit
            - jnp.mean(grad_unit, -1, keepdims=True)
            - unit * jnp.mean(grad_unit * unit, -1, keepdims=True)
        )
        middle_ref[here, :] = grad_middle
        grad_attn = grad_middle.astype(BF)
        down_ref[here, :] = grad_attn
        sums = (
            jnp.sum(grad_attn.astype(F32), 0, keepdims=True),
            jnp.sum(grad * unit, 0, keepdims=True),
            jnp.sum(grad, 0, keepdims=True),
        )
        return tuple(x + y for x, y in zip(carry, sums))

    sums = lax.fori_loop(0, count // tile, middle_back, (zero_row,) * 3)
    for i, value in enumerate(sums + (grad_b_down,)):
        vector_held[0, ring + 2 + i : ring + 3 + i, 0:width] = value
    for i in range(ring):
        here = slice(i * out_rows, (i + 1) * out_rows)
        mid_t[here, :] = dot(wo_all[here, :], down_ref[...], 1, 1).astype(BF)
    g_ref = mid_t

    def g_copy(slot, to):
        return remote(
            g_ref.at[pl.ds(HEADS_AT[to][slot] * hd, hd)],
            g_all.at[slot, :, own],
            gsend.at[slot, to],
            grecv.at[slot, place.shift_to(to) - 1],
            (place.d, to),
        )

    for slot in range(heads_here):
        for to in range(ring):

            @pl.when(m == to)
            def _(slot=slot, to=to):
                row = HEADS_AT[to][slot] * hd
                g_all[slot, :, own] = g_ref[row : row + hd, :]

            @pl.when(m != to)
            def _(slot=slot, to=to):
                g_copy(slot, to).start()

    for j in range(ring):
        here = rows_of(shard_of(j) * out_rows, out_rows, 16)
        wo_share[shard_of(j), 0:out_rows, :] = dot(
            context_ref[here, :], down_ref[...], 1, 0
        ).astype(BF)
        out.copy(0, shard_of(j)).start()
    down.fold_one(0, shard_of(ring - 1))
    up.fold_one(0, shard_of(ring - 1))
    out.fold(0)
    for name in ("v", "qk", "lse", "exact"):
        loads[name].wait()

    def qk_row(h):
        head = place.head(h)
        return head // heads_here, lax.rem(head, heads_here) * 2 * hd

    def qk_copy(h, j):
        shard, row = qk_row(h)
        return remote(
            dqk_send.at[h, :, lanes(place.z(j) * count, count)],
            grad_ref.at[shard, rows_of(row, 2 * hd, 2 * hd)],
            qsend.at[h, j - 1],
            qrecv.at[h, j - 1],
            place.to_z(j),
        )

    v_row = 2 * hd * heads_here

    def v_copy(i, j):
        shard, row, rows, _, row_there = FRESH[i]
        return remote(
            dv_send.at[pl.ds(row_there, rows), lanes(place.z(j) * count, count)],
            grad_ref.at[shard, pl.ds(v_row + row, rows)],
            vsend.at[i, j - 1],
            vrecv.at[i, j - 1],
            place.to_z(j),
        )

    def moved_copy(i):
        to, row, rows, _, row_there = MOVED[i]
        return remote(
            dv_send.at[pl.ds(row_there, rows)],
            first_ref.at[pl.ds(row, rows)],
            fsend.at[0],
            frecv.at[0],
            (place.d, to),
        )

    def send_fresh():
        for i, (shard, row, rows, at, row_there) in enumerate(FRESH):

            @pl.when(m == at)
            def _(i=i, shard=shard, row=row, rows=rows, row_there=row_there):
                for j in range(1, ring):
                    v_copy(i, j).start()
                grad_ref[shard, v_row + row : v_row + row + rows, :] = dv_send[
                    pl.ds(row_there, rows), own
                ]

    def send_reused():
        for i, move in enumerate(MOVED):

            @pl.when(m == move[3])
            def _(i=i):
                moved_copy(i).start()

        for at, row, rows, row_there in KEPT:

            @pl.when(m == at)
            def _(row=row, rows=rows, row_there=row_there):
                first_ref[row : row + rows, :] = dv_send[row_there : row_there + rows, :]

    boundary = length_ref[0]
    block = count
    for h in range(heads_here):
        keys[...] = jnp.transpose(qk_ref[h, hd : 2 * hd, :])
        vals[...] = jnp.transpose(v_ref[hd * h : hd * h + hd, :])
        for j in range(1, ring):
            remote(
                g_ref.at[pl.ds(0, hd)],
                g_all.at[h, :, own],
                gsend.at[h, 0],
                grecv.at[h, j - 1],
                place.to_z(j),
            ).wait_recv()
        delta[...] = jnp.sum(
            g_all[h].astype(F32) * exact_ref[hd * h : hd * h + hd, :], 0, keepdims=True
        )
        for ki in range(ring):
            key_start = ki * block
            key_rows = keys[key_start : key_start + block, :]
            val_rows = vals[key_start : key_start + block, :]
            key_t = qk_ref[h, hd : 2 * hd, key_start : key_start + block]
            grad_k = None
            for qi in range(ki, ring):
                query_start = qi * block
                here = slice(query_start, query_start + block)
                q = qk_ref[h, 0:hd, here]
                g = g_all[h, :, here]
                scores = dot(key_rows, q, 1, 0) - lse_ref[h, :, here]
                if ki == qi:
                    scores = jnp.where(
                        diagonal_mask(scores, key_start, query_start), scores, NEG_LARGE
                    )
                elif key_start < half <= query_start:
                    scores = scores + other_document(boundary, key_start, query_start)
                p = jnp.exp(scores)
                grad_p = dot(val_rows, g, 1, 0)
                grad_s = (p * (grad_p - delta[:, here])).astype(BF)
                part_v = dot(g, p.astype(BF), 1, 1)
                part_k = dot(q, grad_s, 1, 1)
                if grad_k is None:
                    grad_v, grad_k = part_v, part_k
                else:
                    grad_v, grad_k = grad_v + part_v, grad_k + part_k
                part_q = dot(key_t, grad_s, 1, 0)
                if ki == 0:
                    dq[:, here] = part_q
                else:
                    dq[:, here] += part_q
            dqk_send[h, hd : 2 * hd, key_start : key_start + block] = grad_k.astype(BF)
            dv_send[hd * h : hd * h + hd, key_start : key_start + block] = grad_v.astype(BF)
        dqk_send[h, 0:hd, :] = (dq[...] * (hd**-0.5)).astype(BF)
        for j in range(1, ring):
            qk_copy(h, j).start()
        shard, row = qk_row(h)
        grad_ref[shard, rows_of(row, 2 * hd, 2 * hd), :] = dqk_send[h, :, own]
        if h == 0:
            for item in (down, up, out):
                item.fold(1)
        if h == 1:
            send_fresh()
        if h == 2:
            send_reused()
    for item in (down, up, out):
        item.fold(2)
    for h in range(heads_here):
        for j in range(1, ring):
            qk_copy(h, j).wait_recv()
            qk_copy(h, j).wait_send()
    for to in range(ring):

        @pl.when(m != to)
        def _(to=to):
            for slot in range(heads_here):
                g_copy(slot, to).wait_send()

    for i, (shard, row, rows, at, row_there) in enumerate(FRESH):

        @pl.when(m == at)
        def _(i=i):
            for j in range(1, ring):
                v_copy(i, j).wait_send()

        @pl.when(m != at)
        def _(i=i, shard=shard, row=row, rows=rows, at=at, row_there=row_there):
            shift = lax.rem(m - at + ring, ring)
            remote(
                dv_send.at[pl.ds(row_there, rows), own],
                grad_ref.at[shard, pl.ds(v_row + row, rows)],
                vsend.at[i, shift - 1],
                vrecv.at[i, shift - 1],
                place.to_z(shift),
            ).wait_recv()

    for i, move in enumerate(MOVED):

        @pl.when(m == move[3])
        def _(i=i):
            moved_copy(i).wait_send()

        @pl.when(m == move[0])
        def _(i=i):
            moved_copy(i).wait_recv()

    for name in ("normed", "wt"):
        loads[name].wait()
    ones = jnp.ones((8, count), BF)
    for j in range(ring):
        up.copy(0, j).wait_send()
        wu_all[j, 0:pack_lanes, :] = dot(grad_ref[j], normed_ref[...], 1, 0).astype(BF)
        pack.copy(0, j).start()
        sums = dot(ones, grad_ref[j], 1, 1)
        vector_held[0, j : j + 1, 0:pack_lanes] = sums[0:1]

    def input_back(i, carry):
        here = lanes(i * tile, tile)
        grad = None
        for j in range(ring):
            part = dot(grad_ref[j, :, here], wt_all[j], 0, 0)
            grad = part if grad is None else grad + part
        here = rows_of(i * tile, tile, tile)
        value = hidden_ref[here, :]
        center = value - jnp.mean(value, -1, keepdims=True)
        scale = lax.rsqrt(jnp.mean(center * center, -1, keepdims=True) + EPSILON)
        unit = center * scale
        grad_unit = grad * pre_gain_ref[...]
        grad_in_ref[here, :] = middle_ref[here, :] + scale * (
            grad_unit
            - jnp.mean(grad_unit, -1, keepdims=True)
            - unit * jnp.mean(grad_unit * unit, -1, keepdims=True)
        )
        sums = (
            jnp.sum(grad * unit, 0, keepdims=True),
            jnp.sum(grad, 0, keepdims=True),
        )
        return tuple(x + y for x, y in zip(carry, sums))

    sums = lax.fori_loop(0, count // tile, input_back, (zero_row,) * 2)
    for i, value in enumerate(sums):
        vector_held[0, ring + i : ring + 1 + i, 0:width] = value

    routes = [place.to_core, place.to_x, place.to_y]
    routes += [place.to_plane(step) for step in place.steps()]
    bit = 1
    while bit < ring:
        routes.append((place.d, m + bit - 2 * bit * lax.rem(m // bit, 2)))
        bit *= 2

    def vector_copy(k):
        return remote(
            vector_held.at[k], vector_came.at[k], wsend.at[k], wrecv.at[k], routes[k]
        )

    def vector_fold(k):
        vector_copy(k).wait_recv()
        value = vector_held[k] + vector_came[k]
        if k + 1 < len(routes):
            vector_held[k + 1] = value
            vector_copy(k + 1).start()
        else:
            vector_sum[...] = value

    vector_copy(0).start()
    ffn = (down, up, out)
    pack.fold(0)
    for item in ffn:
        item.fold_pair()
    vector_fold(0)
    pack.fold(1)
    for item in ffn:
        item.finish_sum()
    vector_fold(1)
    pack.fold(2)
    vector_fold(2)
    for item in ffn:
        item.spread(6)
    pack.fold_pair()
    for k in range(3, len(routes) - 1):
        vector_fold(k)
    for item in ffn:
        item.spread(7)
    pack.finish_sum()
    vector_fold(len(routes) - 1)
    pack.spread(6)
    pack.spread(7)
    everything = (down, up, out, pack)
    for item in everything:
        item.wait(7)
        item.drain(1 if item is up else 0)
    for k in range(len(routes)):
        vector_copy(k).wait_send()


def backward_call(
    ring, heads_here, planes, length, context, hidden, grad_out, pre_gain, rows, bias,
    qk, v, lse, exact, normed, wt, wo, wo_far, wu, wu_far, wd, wd_far, piece,
):
    count, width = hidden.shape
    total = ring * count
    hd = HEAD_DIM
    others = ring - 1
    sds = jax.ShapeDtypeStruct
    dma = pltpu.SemaphoreType.DMA
    hops = 3 + (planes.bit_length() - 1) + (ring.bit_length() - 1)
    stages = 8 + planes.bit_length() - 1
    pack_rows = wt.shape[1]
    out_pad = wo.shape[0] + -wo.shape[0] % (16 * PLANE)
    sizes = [wd.shape[0], wu.shape[0], out_pad, pack_rows]
    bufs = [buf for rows_ in sizes for buf in Reduce.buffers(rows_, width, planes)]
    vector = (ring + 6 + -(ring + 6) % 8, bias.shape[2])
    vm = pltpu.VMEM
    return pl.pallas_call(
        functools.partial(backward_kernel, ring, heads_here, planes),
        out_shape=(
            sds(hidden.shape, F32),
            sds(hidden.shape, F32),
            sds((piece, total), BF),
            sds(wt.shape[1:], BF),
            sds((out_pad, width), BF),
            sds(wu.shape, BF),
            sds(wd.shape, BF),
            sds(vector, F32),
        ),
        in_specs=[SM] + [VM] * 6 + [ANY] * 12,
        out_specs=[VM] * 8,
        scratch_shapes=[
            vm(qk.shape, BF),
            vm(v.shape, BF),
            vm(lse.shape, F32),
            vm(exact.shape, F32),
            vm(normed.shape, BF),
            vm(wt.shape, BF),
            vm((ring * wo.shape[0], width), BF),
            vm((ring,) + wu.shape, BF),
            vm((ring,) + wd.shape, BF),
            vm((count, width), F32),
            vm((count, width), BF),
            vm((width, count), BF),
            vm((count, width), BF),
            vm((width, count), BF),
            vm((count, width), BF),
            vm((count, width), BF),
            vm((ring, out_pad, width), BF),
            vm((heads_here, hd, total), BF),
            vm((total, hd), BF),
            vm((total, hd), BF),
            vm((1, total), F32),
            vm((hd, total), F32),
            vm((heads_here, 2 * hd, total), BF),
            vm((heads_here * hd, total), BF),
            vm((ring, pack_rows, count), BF),
            vm((hops,) + vector, F32),
            vm((hops,) + vector, F32),
            dma((3 * ring + 6,)),
            dma((heads_here, ring)),
            dma((heads_here, others)),
            dma((heads_here, others)),
            dma((heads_here, others)),
            dma((len(FRESH), others)),
            dma((len(FRESH), others)),
            dma((1,)),
            dma((1,)),
            dma((4, stages, ring)),
            dma((4, stages, ring)),
            dma((hops,)),
            dma((hops,)),
        ]
        + bufs,
        compiler_params=pltpu.CompilerParams(
            collective_id=1, has_side_effects=True, vmem_limit_bytes=67043328
        ),
        name="backward",
    )(
        length, context, hidden, grad_out, pre_gain, rows, bias, qk, v, lse, exact,
        normed, wt, wo, wo_far, wu, wu_far, wd, wd_far,
    )


def shards(
    hidden_in,
    first_values,
    first_length,
    pre_gain,
    pre_shift,
    w_query,
    b_query,
    w_key,
    w_value,
    b_value,
    w_out,
    b_out,
    mid_gain,
    mid_shift,
    w_up,
    b_up,
    w_down,
    b_down,
    grad_out,
):
    ring = lax.axis_size("mp")
    m = lax.axis_index("mp")
    hd = HEAD_DIM
    count, width = hidden_in.shape
    head_width = w_query.shape[1]
    heads_here = head_width // hd
    piece = w_value.shape[1]
    pack_rows = 2 * hd * (heads_here + 1)
    wq = w_query.T.reshape(heads_here, 1, hd, width)
    wk = w_key.T.reshape(heads_here, 1, hd, width)
    spare = pack_rows - 2 * head_width - piece
    wt = jnp.concatenate(
        [
            jnp.concatenate([wq, wk], 1).reshape(2 * head_width, width),
            w_value.T,
            jnp.zeros((spare, width), BF),
        ],
        0,
    )
    bq = b_query.reshape(heads_here, 1, hd)
    bias = jnp.concatenate(
        [
            jnp.concatenate([bq, jnp.zeros_like(bq)], 1).reshape(-1),
            b_value,
            jnp.zeros((spare,), F32),
            b_up,
        ]
    )
    bias = jnp.broadcast_to(bias[None], (8, bias.shape[0]))
    context_t, normed, qk, v, lse, exact, wt_all, bias_all, wo_far, wu_far, wd_far = forward_call(
        ring,
        heads_here,
        first_length,
        hidden_in,
        pre_gain[None],
        pre_shift[None],
        wt,
        bias,
        first_values.T,
        w_out,
        w_up,
        w_down,
    )
    rows = jnp.stack([b_out, mid_gain, mid_shift, b_down] * 2)
    layer_out, grad_input, grad_first, pack_sum, wo_sum, wu_sum, wd_sum, vector = backward_call(
        ring,
        heads_here,
        lax.axis_size("dp") // PLANE,
        first_length,
        context_t,
        hidden_in,
        grad_out,
        pre_gain[None],
        rows,
        bias_all,
        qk,
        v,
        lse,
        exact,
        normed,
        wt_all,
        w_out,
        wo_far,
        w_up,
        wu_far,
        w_down,
        wd_far,
        piece,
    )
    own_vector = lax.dynamic_index_in_dim(vector, m, 0, False)
    qk_grad = pack_sum[: 2 * head_width].astype(F32).reshape(heads_here, 2, hd, width)
    v_grad = pack_sum[2 * head_width : 2 * head_width + piece].astype(F32)
    rows = [vector[ring + i, :width] for i in range(6)]
    return (
        layer_out,
        grad_input,
        grad_first.astype(F32).T,
        rows[0],
        rows[1],
        qk_grad[:, 0].reshape(head_width, width).T,
        own_vector[: 2 * head_width].reshape(heads_here, 2, hd)[:, 0].reshape(-1),
        qk_grad[:, 1].reshape(head_width, width).T,
        v_grad.T,
        own_vector[2 * head_width : 2 * head_width + piece],
        wo_sum[:head_width].astype(F32),
        rows[2],
        rows[3],
        rows[4],
        wu_sum.astype(F32),
        own_vector[pack_rows:],
        wd_sum.astype(F32).T,
        rows[5],
    )


def solution(mesh):
    rows, cols = P(("dp", "mp"), None), P(None, "mp")
    return jax.shard_map(
        shards,
        mesh=mesh,
        in_specs=(
            rows,
            P("dp", "mp"),
            P("dp"),
            P(),
            P(),
            cols,
            P("mp"),
            cols,
            cols,
            P("mp"),
            P("mp", None),
            P(),
            P(),
            P(),
            cols,
            P("mp"),
            P("mp", None),
            P(),
            rows,
        ),
        out_specs=(
            rows,
            rows,
            P("dp", "mp"),
            P(),
            P(),
            cols,
            P("mp"),
            cols,
            cols,
            P("mp"),
            P("mp", None),
            P(),
            P(),
            P(),
            cols,
            P("mp"),
            P("mp", None),
            P(),
        ),
        check_vma=False,
    )
```

profile of v0, /device:TPU:0, one launch (start us, length us, event | category | flops | bytes accessed | tf_op | source)
XLA Modules:
  0.0 311.0 jit_solution(738577136850282995)
XLA Ops:
  0.7 0.0 copy-start.12
  0.7 0.0 copy-start.13
  0.7 0.0 copy-start.11
  0.7 0.0 copy-start.6
  0.7 1.3 broadcast_in_dim.20.gain_ref.pre_gain_ref
  2.6 1.1 pad_maximum_fusion
  3.8 0.1 pad.3.clone
  3.8 2.0 maximum_maximum_fusion.wt_ref
  5.8 0.0 copy-done.12
  5.8 0.1 reshape.68
  5.9 0.1 reshape.69
  6.0 0.0 copy-done.13
  6.0 0.0 copy-done.11
  6.0 0.1 concatenate.15
  6.1 0.6 broadcast_in_dim.24.bias_ref
  6.7 0.0 copy-done.6
  6.7 0.6 broadcast_in_dim.21.shift_ref
  7.3 0.0 copy-start.7
  7.3 0.0 copy-start.8
  7.3 128.4 %forward.1 = (bf16[768,512]{1,0:T(8,128)(2,1)}, bf16[512,768]{1,0:T(8,128)(2,1)}, bf16[3,128,2048]{2,1,0:T(8,128)(2,1)}, bf16[192,2048]{1,0:T(8,128)(2,1)}, f32[...) custom-call(s32[1]{0:T(128)S(6)} %copy.42.length_ref, ...), custom_call_target="tpu_custom_call" | custom-call | tf_op jit(solution)/shard_map/forward/pallas_call | solution.py:620
  135.7 0.0 copy-done.7
  135.7 0.0 copy-done.8
  135.7 0.0 copy-done.9
  135.8 0.0 copy-done.10
  135.8 0.7 stack.23.rows_ref
  136.4 157.9 %backward.1 = (f32[512,768]{1,0:T(8,128)}, f32[512,768]{1,0:T(8,128)}, bf16[96,2048]{1,0:T(8,128)(2,1)}, bf16[512,768]{1,0:T(8,128)(2,1)}, bf16[256,768]{1,0:T(8...) custom-call(s32[1]{0:T(128)S(6)} %copy.42.length_ref, ...), custom_call_target="tpu_custom_call" | custom-call | tf_op jit(solution)/shard_map/backward/pallas_call | solution.py:1182
  294.3 1.4 convert_bitcast_fusion
  295.7 0.0 copy-start.2
  295.8 2.0 copy.39
  297.7 0.0 copy-done.2
  297.7 1.6 convert_element_type.5
  299.3 0.0 copy-done.3
  299.3 0.0 copy-start.5
  299.3 1.1 fusion
  300.5 0.0 copy-done.4
  300.5 0.9 convert_bitcast_fusion.1
  301.4 0.0 copy-done.5
  301.4 0.9 slice_convert_fusion
  302.3 0.7 convert_bitcast_fusion.2
  303.0 1.6 slice_reduce_fusion
  304.6 0.7 dynamic-slice_reduce_fusion.1
  305.4 0.1 reshape.72
  305.5 0.6 reshape_squeeze.10
  306.1 1.3 dynamic-slice_bitcast_fusion
  307.4 0.0 copy-done.1
  307.4 1.1 copy.43
  308.6 0.8 copy-done
  309.4 1.1 copy.44
  (15 shorter events, 0.1 us)
Async XLA Ops:
  0.7 5.2 %copy-start.12 = (f32[192]{0:T(256)S(1)}, f32[192]{0:T(256)}, u32[]{:S(2)}) copy-start(f32[192]{0:T(256)} %param.25) | copy-start | bytes 2308
  0.7 5.3 %copy-start.13 = (f32[96]{0:T(128)S(1)}, f32[96]{0:T(128)}, u32[]{:S(2)}) copy-start(f32[96]{0:T(128)} %param.28) | copy-start | bytes 1156
  0.7 5.3 %copy-start.11 = (f32[768]{0:T(1024)S(1)}, f32[768]{0:T(1024)}, u32[]{:S(2)}) copy-start(f32[768]{0:T(1024)} %param.34) | copy-start | bytes 9220
  0.7 6.0 %copy-start.6 = (f32[768]{0:T(1024)S(1)}, f32[768]{0:T(1024)}, u32[]{:S(2)}) copy-start(f32[768]{0:T(1024)} %param.23) | copy-start | bytes 9220
  7.3 128.4 %copy-start.7 = (f32[768]{0:T(1024)S(1)}, f32[768]{0:T(1024)}, u32[]{:S(2)}) copy-start(f32[768]{0:T(1024)} %param.30) | copy-start | bytes 9220
  7.3 128.4 %copy-start.8 = (f32[768]{0:T(1024)S(1)}, f32[768]{0:T(1024)}, u32[]{:S(2)}) copy-start(f32[768]{0:T(1024)} %param.31) | copy-start | bytes 9220
  7.3 128.4 %copy-start.9 = (f32[768]{0:T(1024)S(1)}, f32[768]{0:T(1024)}, u32[]{:S(2)}) copy-start(f32[768]{0:T(1024)} %param.32) | copy-start | bytes 9220
  7.3 128.5 %copy-start.10 = (f32[768]{0:T(1024)S(1)}, f32[768]{0:T(1024)}, u32[]{:S(2)}) copy-start(f32[768]{0:T(1024)} %param.36) | copy-start | bytes 9220
  295.7 2.0 copy-start.2
  297.7 1.6 copy-start.3
  299.3 1.2 copy-start.4
  299.3 2.1 copy-start.5
  300.5 7.0 %copy-start.1 = (f32[512,768]{1,0:T(8,128)S(1)}, f32[512,768]{1,0:T(8,128)}, u32[]{:S(2)}) copy-start(f32[512,768]{1,0:T(8,128)} %get-tuple-element.101) | copy-start | bytes 4718596
  307.4 2.0 copy-start
where the time goes:
time: 314 us; the launch traced here: 311 us
  Pallas kernels  286 us (91%)
  local copies, waits for them, and re-layouts  14.2 us (5%)
  other arithmetic  8.65 us (3%)
    pallas_call x1, Pallas kernels, backward_call(): pl.pallas_call(functools.partial(backward_kernel, ring, heads_here, plane...  158 us
    pallas_call x1, Pallas kernels, forward_call(): pl.pallas_call(functools.partial(forward_kernel, ring, heads_here), out_s...  128 us

commit v1 on v0

--- a/solution.py
+++ b/solution.py
@@ -20,10 +20,17 @@
 LANE = 128
 PLANE = 8
 RING = 4
-HEADS_AT = ((0, 1, 6), (2, 7, 8), (3, 9, 10), (4, 5, 11))
-FRESH = ((0, 0, 96, 0, 0), (1, 0, 32, 0, 96), (1, 32, 64, 1, 0), (2, 0, 64, 2, 0), (2, 64, 32, 3, 0), (3, 0, 96, 3, 32))
-KEPT = ((0, 0, 64, 128), (1, 0, 96, 96), (2, 0, 96, 64), (3, 32, 64, 128))
-MOVED = ((0, 64, 32, 1, 64), (3, 0, 32, 2, 160))
+HEADS_AT = ((0, 1, 6), (7, 8, 2), (9, 10, 3), (4, 5, 11))
+FRESH = (
+    (0, 0, 96, 0, 0),
+    (1, 0, 32, 0, 96),
+    (1, 32, 64, 1, 128),
+    (2, 0, 64, 2, 128),
+    (2, 64, 32, 3, 0),
+    (3, 0, 96, 3, 32),
+)
+KEPT = ((0, 0, 64, 128), (1, 0, 96, 32), (2, 0, 96, 0), (3, 32, 64, 128))
+MOVED = ((0, 64, 32, 1, 0), (3, 0, 32, 2, 96))
 
 
 def dot(left, right, left_dim, right_dim):
@@ -81,10 +88,14 @@
         return lax.rem(position - self.m + self.ring, self.ring)
 
     def head(self, slot):
-        value = HEADS_AT[RING - 1][slot]
-        for k in range(RING - 1):
-            value = jnp.where(self.m == k, HEADS_AT[k][slot], value)
+        value = 0
+        for k, heads in enumerate(HEADS_AT):
+            for at, head in enumerate(heads):
+                value = jnp.where(jnp.logical_and(self.m == k, slot == at), head, value)
         return value
+
+    def shard(self, slot):
+        return self.head(slot) // len(HEADS_AT[0])
 
     def steps(self):
         return [PLANE << b for b in range(self.planes.bit_length() - 1)]
@@ -178,8 +189,9 @@
 
 
 class Reduce:
-    def __init__(self, place, src, bufs, out, send, recv, item, x_first):
+    def __init__(self, place, src, bufs, out, send, recv, item, x_first, first_row=0):
         self.place, self.src, self.out = place, src, out
+        self.first_row = first_row
         self.r_core, self.r_far, self.r_near, self.r_z, self.r_plane = bufs
         self.send, self.recv, self.item, self.x_first = send, recv, item, x_first
         self.part = out.shape[0] // PLANE
@@ -196,7 +208,8 @@
     def copy(self, stage, k):
         place = self.place
         if stage == 0:
-            src = self.src.at[k, self.rows((1 - place.core) * 4, 4)]
+            begin = self.first_row + (1 - place.core) * 4 * self.part
+            src = self.src.at[k, rows_of(begin, 4 * self.part, self.part & -self.part)]
             dst, target = self.r_core.at[k], place.to_core
         elif stage == 1:
             src = self.r_core.at[k, self.rows((1 - self.far_bit) * 2, 2)]
@@ -237,7 +250,8 @@
     def fold_one(self, stage, k):
         place, part = self.place, self.part
         if stage == 0:
-            kept, base, into, size = self.src, place.core * 4 * part, self.r_core, 4 * part
+            base = self.first_row + place.core * 4 * part
+            kept, into, size = self.src, self.r_core, 4 * part
         elif stage == 1:
             kept, base, into, size = self.r_core, self.far_bit * 2 * part, self.r_far, 2 * part
         else:
@@ -417,16 +431,16 @@
         def _(row=row, rows=rows, row_there=row_there):
             v_ref[row_there : row_there + rows, :] = first_ref[row : row + rows, :]
 
-    for item in big:
-        item.start(0)
-
     normed_ref[...] = layer_norm(hidden_ref[...], gain_ref[...], shift_ref[...]).astype(BF)
     wt_all[m] = wt_ref[...]
     bias_all[m] = bias_ref[...]
 
-    for stage in (1, 2):
-        for item in small:
-            item.start(stage)
+    for item in small:
+        item.start(1)
+    for item in big:
+        item.start(0)
+    for item in small:
+        item.start(2)
     for item in big:
         item.start(1)
     for stage in (3, 4):
@@ -458,15 +472,19 @@
             (place.d, to),
         )
 
-    where_is = {head: (to, slot) for to, heads in enumerate(HEADS_AT) for slot, head in enumerate(heads)}
+    where_is = {
+        (head // heads_here, slot): to
+        for to, heads in enumerate(HEADS_AT)
+        for slot, head in enumerate(heads)
+    }
     v_row = 2 * hd * heads_here
 
     for shard in range(ring):
         out = dot(wt_all[shard], normed_ref[...], 1, 1)
         out = out + jnp.transpose(bias_all[shard, :, 0:pack_rows])[:, 0:1]
-        for i in range(heads_here):
-            to, slot = where_is[heads_here * shard + i]
-            row = 2 * hd * i
+        for slot in range(heads_here):
+            to = where_is[shard, slot]
+            row = 2 * hd * slot
             y_send[to, slot, 0:hd, :] = (out[row : row + hd] * (hd**-0.5)).astype(BF)
             y_send[to, slot, hd : 2 * hd, :] = out[row + hd : row + 2 * hd].astype(BF)
         vy_send[shard] = out[v_row : v_row + piece].astype(BF)
@@ -495,6 +513,9 @@
 
     for slot in range(1, heads_here):
         share(slot)
+    for stage in (2, 3):
+        for item in big:
+            item.start(stage)
 
     def qk_arrive(slot):
         for shift in range(1, ring):
@@ -506,7 +527,6 @@
                 place.to_z(shift),
             ).wait_recv()
 
-    qk_arrive(0)
     for i, (shard, row, rows, to, row_there) in enumerate(FRESH):
 
         @pl.when(m == to)
@@ -531,24 +551,25 @@
 
     def context_copy(h, j):
         return remote(
-            c_send.at[pl.ds(hd * h, hd), lanes(place.z(j) * count, count)],
+            c_send.at[rows_of(hd * h, hd, hd), lanes(place.z(j) * count, count)],
             context_ref.at[rows_of(place.head(h) * hd, hd, hd)],
             csend.at[h, j - 1],
             crecv.at[h, j - 1],
             place.to_z(j),
         )
 
-    for h in range(heads_here):
-        if h > 0:
-            qk_arrive(h)
+    def attend(h, carry):
+        qk_arrive(h)
+        here_h = rows_of(hd * h, hd, hd)
         keys[...] = jnp.transpose(qk_ref[h, hd : 2 * hd, :])
         for qi in range(ring):
             query_start = qi * block
-            q = qk_ref[h, 0:hd, query_start : query_start + block]
+            queries = slice(query_start, query_start + block)
+            q = qk_ref[h, 0:hd, queries]
             top = None
             for ki in range(qi + 1):
                 key_start = ki * block
-                v = v_ref[hd * h : hd * h + hd, key_start : key_start + block]
+                v = v_ref[here_h, key_start : key_start + block]
                 scores = dot(keys[key_start : key_start + block, :], q, 1, 0)
                 if ki == qi:
                     scores = jnp.where(
@@ -569,15 +590,21 @@
                     running = running * factor + part
                 top = new_top
             result = running / run_sum
-            exact_ref[hd * h : hd * h + hd, query_start : query_start + block] = result
-            c_send[hd * h : hd * h + hd, query_start : query_start + block] = result.astype(BF)
-            lse_ref[h, :, query_start : query_start + block] = top + jnp.log(run_sum)
+            exact_ref[here_h, queries] = result
+            c_send[here_h, queries] = result.astype(BF)
+            lse_ref[h, :, queries] = top + jnp.log(run_sum)
         for j in range(1, ring):
             context_copy(h, j).start()
-        context_ref[rows_of(place.head(h) * hd, hd, hd), :] = c_send[hd * h : hd * h + hd, own]
-        for item in big:
-            item.start(2 + h)
-
+        context_ref[rows_of(place.head(h) * hd, hd, hd), :] = c_send[here_h, own]
+
+        @pl.when(h == 1)
+        def _():
+            for item in big:
+                item.start(4)
+
+        return carry
+
+    lax.fori_loop(0, heads_here, attend, 0)
     for item in big:
         item.arrive()
     for h in range(heads_here):
@@ -694,7 +721,6 @@
     v_ref,
     lse_ref,
     exact_ref,
-    normed_ref,
     wt_all,
     wo_all,
     wu_all,
@@ -706,14 +732,13 @@
     down_t,
     act_ref,
     gup_ref,
+    g_ref,
     wo_share,
     g_all,
     keys,
     vals,
     delta,
     dq,
-    dqk_send,
-    dv_send,
     grad_ref,
     vector_held,
     vector_came,
@@ -764,7 +789,6 @@
     load("qk", qk_hbm, qk_ref)
     load("lse", lse_hbm, lse_ref)
     load("exact", exact_hbm, exact_ref)
-    load("normed", normed_hbm, normed_ref)
     load("wt", wt_hbm, wt_all)
     place.barrier()
 
@@ -772,7 +796,7 @@
         return rows_ref[i : i + 1, :]
 
     b_out, mid_gain, mid_shift, b_down = row(0), row(1), row(2), row(3)
-    act_ref[...] = jnp.transpose(context_ref[...])
+    act_ref[0] = jnp.transpose(context_ref[...])
     vector_held[0] = jnp.zeros_like(vector_held[0])
     wo_share[:, out_rows:, :] = jnp.zeros_like(wo_share[:, out_rows:, :])
     grad_ref[:, 2 * hd * heads_here + piece :, :] = jnp.zeros_like(
@@ -783,7 +807,7 @@
 
     def project(i, carry):
         here = rows_of(i * tile, tile, tile)
-        attended = dot(act_ref[here, :], wo_all[...], 1, 0) + b_out
+        attended = dot(act_ref[0, here, :], wo_all[...], 1, 0) + b_out
         middle = hidden_ref[here, :] + attended
         middle_ref[here, :] = middle
         layer_ref[here, :] = middle + b_down
@@ -801,21 +825,34 @@
     down = Reduce(place, wd_all, bufs[0:5], wd_sum, rsend, rrecv, 0, False)
     up = Reduce(place, wu_all, bufs[5:10], wu_sum, rsend, rrecv, 1, True)
     out = Reduce(place, wo_share, bufs[10:15], wo_sum, rsend, rrecv, 2, True)
-    pack = Reduce(
-        place, wu_all.at[:, pl.ds(0, pack_lanes)], bufs[15:20], pack_sum, rsend, rrecv, 3, True
-    )
+    group = 2 * hd
+    packs = [
+        Reduce(
+            place,
+            wu_all,
+            bufs[15 + 5 * i : 20 + 5 * i],
+            pack_sum.at[pl.ds(group * i, group)],
+            rsend,
+            rrecv,
+            3 + i,
+            i % 2 == 0,
+            group * i,
+        )
+        for i in range(heads_here + 1)
+    ]
 
     big = count // 2
-    for j in range(ring):
-        loads[("wu", j)].wait()
-        loads[("wd", j)].wait()
+
+    def feed_shard(j, carry):
         s = shard_of(j)
+        for i, hbm, ref in ((0, wu_hbm, wu_all), (1, wd_hbm, wd_all)):
+            pltpu.make_async_copy(hbm, ref.at[s], lsem.at[ring + 2 * j + i]).wait()
         b_up = bias_ref[s, 0:1, pack_lanes:]
 
-        def feed(i, carry, j=s, b_up=b_up):
+        def feed(i, carry):
             here = rows_of(i * big, big, big)
-            u = dot(mid_ref[here, :], wu_all[j], 1, 0) + b_up
-            grad_act = dot(down_ref[here, :], wd_all[j], 1, 1)
+            u = dot(mid_ref[here, :], wu_all[s], 1, 0) + b_up
+            grad_act = dot(down_ref[here, :], wd_all[s], 1, 1)
             square = u * u
             t = jnp.tanh(0.7978845608028654 * (u + 0.044715 * u * square))
             act = (0.5 * u * (1.0 + t)).astype(BF)
@@ -823,27 +860,18 @@
                 1.0 + 0.134145 * square
             )
             grad_up = (grad_act * slope).astype(BF)
-            act_ref[here, :] = act
-            gup_ref[here, :] = grad_up
-            layer_ref[here, :] += dot(act, wd_all[j], 1, 0)
-            grad_in_ref[here, :] += dot(grad_up, wu_all[j], 1, 1)
+            act_ref[s, here, :] = act
+            gup_ref[s, here, :] = grad_up
+            layer_ref[here, :] += dot(act, wd_all[s], 1, 0)
+            grad_in_ref[here, :] += dot(grad_up, wu_all[s], 1, 1)
             return carry + jnp.sum(grad_up.astype(F32), 0, keepdims=True)
 
         grad_b_up = lax.fori_loop(0, count // big, feed, jnp.zeros((1, wu_all.shape[2]), F32))
         vector_held[0, pl.ds(s, 1), pack_lanes:] = grad_b_up
-
-        def weigh(i, carry, j=s):
-            here = lanes(i * 256, 256)
-            wu_all[j, :, here] = dot(mid_t[...], gup_ref[:, here], 1, 0).astype(BF)
-            wd_all[j, :, here] = dot(down_t[...], act_ref[:, here], 1, 0).astype(BF)
-            return carry
-
-        lax.fori_loop(0, wu_all.shape[2] // 256, weigh, 0)
-        down.copy(0, s).start()
-        up.copy(0, s).start()
-        if j > 0:
-            down.fold_one(0, shard_of(j - 1))
-            up.fold_one(0, shard_of(j - 1))
+        return carry
+
+    lax.fori_loop(0, ring, feed_shard, 0)
+    load("normed", normed_hbm, mid_ref)
 
     def middle_back(i, carry):
         here = rows_of(i * tile, tile, tile)
@@ -873,8 +901,7 @@
         vector_held[0, ring + 2 + i : ring + 3 + i, 0:width] = value
     for i in range(ring):
         here = slice(i * out_rows, (i + 1) * out_rows)
-        mid_t[here, :] = dot(wo_all[here, :], down_ref[...], 1, 1).astype(BF)
-    g_ref = mid_t
+        g_ref[here, :] = dot(wo_all[here, :], down_ref[...], 1, 1).astype(BF)
 
     def g_copy(slot, to):
         return remote(
@@ -903,21 +930,38 @@
             context_ref[here, :], down_ref[...], 1, 0
         ).astype(BF)
         out.copy(0, shard_of(j)).start()
+
+    def weigh_shard(j, carry):
+        s = shard_of(j)
+
+        def weigh(i, carry):
+            here = lanes(i * 256, 256)
+            wu_all[s, :, here] = dot(mid_t[...], gup_ref[s, :, here], 1, 0).astype(BF)
+            wd_all[s, :, here] = dot(down_t[...], act_ref[s, :, here], 1, 0).astype(BF)
+            return carry
+
+        lax.fori_loop(0, wu_all.shape[2] // 256, weigh, 0)
+        down.copy(0, s).start()
+        up.copy(0, s).start()
+
+        @pl.when(j > 0)
+        def _():
+            down.fold_one(0, shard_of(j - 1))
+            up.fold_one(0, shard_of(j - 1))
+
+        return carry
+
+    lax.fori_loop(0, ring, weigh_shard, 0)
+    out.fold(0)
     down.fold_one(0, shard_of(ring - 1))
     up.fold_one(0, shard_of(ring - 1))
-    out.fold(0)
     for name in ("v", "qk", "lse", "exact"):
         loads[name].wait()
 
-    def qk_row(h):
-        head = place.head(h)
-        return head // heads_here, lax.rem(head, heads_here) * 2 * hd
-
     def qk_copy(h, j):
-        shard, row = qk_row(h)
         return remote(
-            dqk_send.at[h, :, lanes(place.z(j) * count, count)],
-            grad_ref.at[shard, rows_of(row, 2 * hd, 2 * hd)],
+            qk_ref.at[h, :, lanes(place.z(j) * count, count)],
+            grad_ref.at[place.shard(h), rows_of(2 * hd * h, 2 * hd, 2 * hd)],
             qsend.at[h, j - 1],
             qrecv.at[h, j - 1],
             place.to_z(j),
@@ -928,7 +972,7 @@
     def v_copy(i, j):
         shard, row, rows, _, row_there = FRESH[i]
         return remote(
-            dv_send.at[pl.ds(row_there, rows), lanes(place.z(j) * count, count)],
+            v_ref.at[pl.ds(row_there, rows), lanes(place.z(j) * count, count)],
             grad_ref.at[shard, pl.ds(v_row + row, rows)],
             vsend.at[i, j - 1],
             vrecv.at[i, j - 1],
@@ -938,21 +982,23 @@
     def moved_copy(i):
         to, row, rows, _, row_there = MOVED[i]
         return remote(
-            dv_send.at[pl.ds(row_there, rows)],
+            v_ref.at[pl.ds(row_there, rows)],
             first_ref.at[pl.ds(row, rows)],
             fsend.at[0],
             frecv.at[0],
             (place.d, to),
         )
 
-    def send_fresh():
+    def send_fresh(slot):
         for i, (shard, row, rows, at, row_there) in enumerate(FRESH):
+            if (row_there + rows > 2 * hd) != (slot == 2):
+                continue
 
             @pl.when(m == at)
             def _(i=i, shard=shard, row=row, rows=rows, row_there=row_there):
                 for j in range(1, ring):
                     v_copy(i, j).start()
-                grad_ref[shard, v_row + row : v_row + row + rows, :] = dv_send[
+                grad_ref[shard, v_row + row : v_row + row + rows, :] = v_ref[
                     pl.ds(row_there, rows), own
                 ]
 
@@ -967,13 +1013,45 @@
 
             @pl.when(m == at)
             def _(row=row, rows=rows, row_there=row_there):
-                first_ref[row : row + rows, :] = dv_send[row_there : row_there + rows, :]
+                first_ref[row : row + rows, :] = v_ref[row_there : row_there + rows, :]
+
+    ones = jnp.ones((8, count), BF)
+
+    def process(i):
+        if i == 0:
+            for name in ("normed", "wt"):
+                loads[name].wait()
+            for k in range(ring):
+                up.copy(0, k).wait_send()
+        if i < heads_here:
+            for j in range(1, ring):
+                qk_copy(i, j).wait_recv()
+        begin = group * i
+        here = slice(begin, begin + group)
+        for k in range(ring):
+            wu_all[k, here, :] = dot(grad_ref[k, here, :], mid_ref[...], 1, 0).astype(BF)
+            packs[i].copy(0, k).start()
+        for k in range(ring):
+            sums = dot(ones, grad_ref[k, here, :], 1, 1)
+            vector_held[0, k : k + 1, here] = sums[0:1]
+        weights = jnp.concatenate([wt_all[k, here, :] for k in range(ring)], 0)
+
+        def add(t, carry):
+            toks = lanes(t * tile, tile)
+            grads = jnp.concatenate([grad_ref[k, here, toks] for k in range(ring)], 0)
+            part = dot(grads, weights, 0, 0)
+            rows = rows_of(t * tile, tile, tile)
+            grad_in_ref[rows, :] = part if i == 0 else grad_in_ref[rows, :] + part
+            return carry
+
+        lax.fori_loop(0, count // tile, add, 0)
 
     boundary = length_ref[0]
     block = count
-    for h in range(heads_here):
+    def attend_back(h, carry):
+        here_h = rows_of(hd * h, hd, hd)
         keys[...] = jnp.transpose(qk_ref[h, hd : 2 * hd, :])
-        vals[...] = jnp.transpose(v_ref[hd * h : hd * h + hd, :])
+        vals[...] = jnp.transpose(v_ref[here_h, :])
         for j in range(1, ring):
             remote(
                 g_ref.at[pl.ds(0, hd)],
@@ -983,7 +1061,7 @@
                 place.to_z(j),
             ).wait_recv()
         delta[...] = jnp.sum(
-            g_all[h].astype(F32) * exact_ref[hd * h : hd * h + hd, :], 0, keepdims=True
+            g_all[h].astype(F32) * exact_ref[here_h, :], 0, keepdims=True
         )
         for ki in range(ring):
             key_start = ki * block
@@ -1017,26 +1095,34 @@
                     dq[:, here] = part_q
                 else:
                     dq[:, here] += part_q
-            dqk_send[h, hd : 2 * hd, key_start : key_start + block] = grad_k.astype(BF)
-            dv_send[hd * h : hd * h + hd, key_start : key_start + block] = grad_v.astype(BF)
-        dqk_send[h, 0:hd, :] = (dq[...] * (hd**-0.5)).astype(BF)
+            qk_ref[h, hd : 2 * hd, key_start : key_start + block] = grad_k.astype(BF)
+            v_ref[here_h, key_start : key_start + block] = grad_v.astype(BF)
+        qk_ref[h, 0:hd, :] = (dq[...] * (hd**-0.5)).astype(BF)
         for j in range(1, ring):
             qk_copy(h, j).start()
-        shard, row = qk_row(h)
-        grad_ref[shard, rows_of(row, 2 * hd, 2 * hd), :] = dqk_send[h, :, own]
-        if h == 0:
-            for item in (down, up, out):
-                item.fold(1)
-        if h == 1:
-            send_fresh()
-        if h == 2:
-            send_reused()
-    for item in (down, up, out):
+        grad_ref[place.shard(h), rows_of(2 * hd * h, 2 * hd, 2 * hd), :] = qk_ref[h, :, own]
+
+        @pl.when(h == 1)
+        def _():
+            send_fresh(1)
+
+        return carry
+
+    lax.fori_loop(0, heads_here, attend_back, 0)
+    send_fresh(2)
+    send_reused()
+    ffn = (down, up, out)
+    for item in ffn:
+        item.fold(1)
+    process(0)
+    process(1)
+    packs[0].fold(0)
+    packs[1].fold(0)
+    packs[0].fold(1)
+    for item in ffn:
         item.fold(2)
-    for h in range(heads_here):
-        for j in range(1, ring):
-            qk_copy(h, j).wait_recv()
-            qk_copy(h, j).wait_send()
+    packs[1].fold(1)
+    packs[0].fold(2)
     for to in range(ring):
 
         @pl.when(m != to)
@@ -1055,7 +1141,7 @@
         def _(i=i, shard=shard, row=row, rows=rows, at=at, row_there=row_there):
             shift = lax.rem(m - at + ring, ring)
             remote(
-                dv_send.at[pl.ds(row_there, rows), own],
+                v_ref.at[pl.ds(row_there, rows), own],
                 grad_ref.at[shard, pl.ds(v_row + row, rows)],
                 vsend.at[i, shift - 1],
                 vrecv.at[i, shift - 1],
@@ -1072,23 +1158,12 @@
         def _(i=i):
             moved_copy(i).wait_recv()
 
-    for name in ("normed", "wt"):
-        loads[name].wait()
-    ones = jnp.ones((8, count), BF)
-    for j in range(ring):
-        up.copy(0, j).wait_send()
-        wu_all[j, 0:pack_lanes, :] = dot(grad_ref[j], normed_ref[...], 1, 0).astype(BF)
-        pack.copy(0, j).start()
-        sums = dot(ones, grad_ref[j], 1, 1)
-        vector_held[0, j : j + 1, 0:pack_lanes] = sums[0:1]
+    process(2)
+    process(3)
 
     def input_back(i, carry):
-        here = lanes(i * tile, tile)
-        grad = None
-        for j in range(ring):
-            part = dot(grad_ref[j, :, here], wt_all[j], 0, 0)
-            grad = part if grad is None else grad + part
         here = rows_of(i * tile, tile, tile)
+        grad = grad_in_ref[here, :]
         value = hidden_ref[here, :]
         center = value - jnp.mean(value, -1, keepdims=True)
         scale = lax.rsqrt(jnp.mean(center * center, -1, keepdims=True) + EPSILON)
@@ -1131,34 +1206,51 @@
             vector_sum[...] = value
 
     vector_copy(0).start()
-    ffn = (down, up, out)
-    pack.fold(0)
+    first, second, third, fourth = packs
+    second.fold(2)
+    third.fold(0)
+    fourth.fold(0)
+    vector_fold(0)
     for item in ffn:
         item.fold_pair()
-    vector_fold(0)
-    pack.fold(1)
+    third.fold(1)
+    fourth.fold(1)
+    vector_fold(1)
+    first.fold_pair()
+    second.fold_pair()
     for item in ffn:
         item.finish_sum()
-    vector_fold(1)
-    pack.fold(2)
+    third.fold(2)
+    fourth.fold(2)
     vector_fold(2)
+    first.finish_sum()
+    second.finish_sum()
+    third.fold_pair()
+    fourth.fold_pair()
     for item in ffn:
         item.spread(6)
-    pack.fold_pair()
     for k in range(3, len(routes) - 1):
         vector_fold(k)
+    first.spread(6)
+    second.spread(6)
+    third.finish_sum()
+    fourth.finish_sum()
     for item in ffn:
         item.spread(7)
-    pack.finish_sum()
     vector_fold(len(routes) - 1)
-    pack.spread(6)
-    pack.spread(7)
-    everything = (down, up, out, pack)
+    for item in packs:
+        item.spread(6 if item in (third, fourth) else 7)
+    third.spread(7)
+    fourth.spread(7)
+    everything = ffn + tuple(packs)
     for item in everything:
         item.wait(7)
         item.drain(1 if item is up else 0)
     for k in range(len(routes)):
         vector_copy(k).wait_send()
+    for h in range(heads_here):
+        for j in range(1, ring):
+            qk_copy(h, j).wait_send()
 
 
 def backward_call(
@@ -1175,7 +1267,7 @@
     stages = 8 + planes.bit_length() - 1
     pack_rows = wt.shape[1]
     out_pad = wo.shape[0] + -wo.shape[0] % (16 * PLANE)
-    sizes = [wd.shape[0], wu.shape[0], out_pad, pack_rows]
+    sizes = [wd.shape[0], wu.shape[0], out_pad] + [2 * hd] * (heads_here + 1)
     bufs = [buf for rows_ in sizes for buf in Reduce.buffers(rows_, width, planes)]
     vector = (ring + 6 + -(ring + 6) % 8, bias.shape[2])
     vm = pltpu.VMEM
@@ -1198,7 +1290,6 @@
             vm(v.shape, BF),
             vm(lse.shape, F32),
             vm(exact.shape, F32),
-            vm(normed.shape, BF),
             vm(wt.shape, BF),
             vm((ring * wo.shape[0], width), BF),
             vm((ring,) + wu.shape, BF),
@@ -1208,16 +1299,15 @@
             vm((width, count), BF),
             vm((count, width), BF),
             vm((width, count), BF),
-            vm((count, width), BF),
-            vm((count, width), BF),
+            vm((ring, count, width), BF),
+            vm((ring, count, width), BF),
+            vm((width, count), BF),
             vm((ring, out_pad, width), BF),
             vm((heads_here, hd, total), BF),
             vm((total, hd), BF),
             vm((total, hd), BF),
             vm((1, total), F32),
             vm((hd, total), F32),
-            vm((heads_here, 2 * hd, total), BF),
-            vm((heads_here * hd, total), BF),
             vm((ring, pack_rows, count), BF),
             vm((hops,) + vector, F32),
             vm((hops,) + vector, F32),
@@ -1230,8 +1320,8 @@
             dma((len(FRESH), others)),
             dma((1,)),
             dma((1,)),
-            dma((4, stages, ring)),
-            dma((4, stages, ring)),
+            dma((3 + heads_here + 1, stages, ring)),
+            dma((3 + heads_here + 1, stages, ring)),
             dma((hops,)),
             dma((hops,)),
         ]
@@ -1275,8 +1365,16 @@
     heads_here = head_width // hd
     piece = w_value.shape[1]
     pack_rows = 2 * hd * (heads_here + 1)
-    wq = w_query.T.reshape(heads_here, 1, hd, width)
-    wk = w_key.T.reshape(heads_here, 1, hd, width)
+    turned = jnp.logical_or(m == 1, m == 2)
+
+    def to_slots(value):
+        return jnp.where(turned, jnp.roll(value, -1, 0), value)
+
+    def from_slots(value):
+        return jnp.where(turned, jnp.roll(value, 1, 0), value)
+
+    wq = to_slots(w_query.T.reshape(heads_here, 1, hd, width))
+    wk = to_slots(w_key.T.reshape(heads_here, 1, hd, width))
     spare = pack_rows - 2 * head_width - piece
     wt = jnp.concatenate(
         [
@@ -1286,7 +1384,7 @@
         ],
         0,
     )
-    bq = b_query.reshape(heads_here, 1, hd)
+    bq = to_slots(b_query.reshape(heads_here, 1, hd))
     bias = jnp.concatenate(
         [
             jnp.concatenate([bq, jnp.zeros_like(bq)], 1).reshape(-1),
@@ -1337,7 +1435,7 @@
         piece,
     )
     own_vector = lax.dynamic_index_in_dim(vector, m, 0, False)
-    qk_grad = pack_sum[: 2 * head_width].astype(F32).reshape(heads_here, 2, hd, width)
+    qk_grad = from_slots(pack_sum[: 2 * head_width].astype(F32).reshape(heads_here, 2, hd, width))
     v_grad = pack_sum[2 * head_width : 2 * head_width + piece].astype(F32)
     rows = [vector[ring + i, :width] for i in range(6)]
     return (
@@ -1347,7 +1445,7 @@
         rows[0],
         rows[1],
         qk_grad[:, 0].reshape(head_width, width).T,
-        own_vector[: 2 * head_width].reshape(heads_here, 2, hd)[:, 0].reshape(-1),
+        from_slots(own_vector[: 2 * head_width].reshape(heads_here, 2, hd))[:, 0].reshape(-1),
         qk_grad[:, 1].reshape(head_width, width).T,
         v_grad.T,
         own_vector[2 * head_width : 2 * head_width + piece],

time: 314 us -> 285 us (0.908)
  Pallas kernels: 286 us -> 254 us
  local copies, waits for them, and re-layouts: 14.2 us -> 19.6 us
    pallas_call x1, Pallas kernels: 128 us -> 104 us  [forward_call(): pl.pallas_call(functools.partial(forward_kernel, ring, heads_here), out_s...]
    pallas_call x1, Pallas kernels: 158 us -> 150 us  [backward_call(): pl.pallas_call(functools.partial(backward_kernel, ring, heads_here, plane...]
    slice x3 -> x10, local copies, waits for them, and re-layouts: 0.8 us -> 4.44 us  [the longest x3 1.96 us: to_slots(): return jnp.where(turned, jnp.roll(value, -1, 0), value)]
where the time goes in v1:
time: 285 us; the launch traced here: 284 us
  Pallas kernels  254 us (89%)
  local copies, waits for them, and re-layouts  19.6 us (7%)
  other arithmetic  8.75 us (3%)
    pallas_call x1, Pallas kernels, backward_call(): pl.pallas_call(functools.partial(backward_kernel, ring, heads_here, plane...  150 us
    pallas_call x1, Pallas kernels, forward_call(): pl.pallas_call(functools.partial(forward_kernel, ring, heads_here), out_s...  104 us
    unnamed x36, local copies, waits for them, and re-layouts  5.74 us

profile of v1, /device:TPU:0, one launch (start us, length us, event | category | flops | bytes accessed | tf_op | source)
XLA Modules:
  0.0 283.8 jit_solution(7403640387010147076)
XLA Ops:
  0.7 0.9 slice.149
  1.6 0.9 slice.151
  2.6 0.9 slice_bitcast_fusion
  3.5 0.9 slice_bitcast_fusion.1
  4.4 1.1 maximum_select_fusion.1
  5.5 0.0 copy-start.14
  5.5 0.0 copy-start.13
  5.5 0.0 copy-start.15
  5.6 0.0 copy-start.7
  5.6 0.0 copy-start.8
  5.6 0.1 pad_maximum_fusion
  5.7 0.1 pad.9.clone
  5.7 1.1 maximum_maximum_fusion.wt_ref
  6.8 0.1 reshape.215
  6.9 0.1 slice.122
  7.0 0.1 concatenate.75
  7.1 0.1 reshape.216
  7.2 0.1 concatenate.79
  7.3 0.6 broadcast_in_dim.24.bias_ref
  7.9 0.6 broadcast_in_dim.20.gain_ref.pre_gain_ref
  9.1 0.6 broadcast_in_dim.21.shift_ref
  9.7 104.4 %forward.1 = (bf16[768,512]{1,0:T(8,128)(2,1)}, bf16[512,768]{1,0:T(8,128)(2,1)}, bf16[3,128,2048]{2,1,0:T(8,128)(2,1)}, bf16[192,2048]{1,0:T(8,128)(2,1)}, f32[...) custom-call(s32[1]{0:T(128)S(6)} %copy.53.length_ref, ...), custom_call_target="tpu_custom_call" | custom-call | tf_op jit(solution)/shard_map/forward/pallas_call | solution.py:647
  114.2 0.0 copy-done.12
  114.2 0.7 stack.23.rows_ref
  114.9 149.5 %backward.1 = (f32[512,768]{1,0:T(8,128)}, f32[512,768]{1,0:T(8,128)}, bf16[96,2048]{1,0:T(8,128)(2,1)}, bf16[512,768]{1,0:T(8,128)(2,1)}, bf16[256,768]{1,0:T(8...) custom-call(s32[1]{0:T(128)S(6)} %copy.53.length_ref, ...), custom_call_target="tpu_custom_call" | custom-call | tf_op jit(solution)/shard_map/backward/pallas_call | solution.py:1274
  264.4 0.7 dynamic-slice_reduce_fusion.1
  265.1 0.1 reshape.218
  265.2 0.7 dynamic-slice_reduce_fusion.2
  265.9 0.1 slice.135
  266.0 0.8 dynamic-slice_reduce_fusion.3
  266.8 0.1 slice.133
  266.9 0.6 reshape_squeeze.10
  267.5 1.1 slice_convert_fusion
  268.7 0.1 slice.154
  268.8 0.1 maximum_select_fusion
  268.9 1.1 fusion.1
  270.0 0.6 copy-done.3
  270.6 0.2 convert_bitcast_fusion
  270.8 2.0 copy.49
  272.8 1.6 convert_element_type.14
  274.3 1.0 convert_bitcast_fusion.1
  275.3 0.9 slice_convert_fusion.1
  276.2 1.6 convert_bitcast_fusion.2
  277.8 1.6 slice_reduce_fusion
  279.4 1.3 dynamic-slice_bitcast_fusion
  280.7 1.1 copy.54
  281.9 0.8 copy-done
  282.7 1.1 copy.55
  (36 shorter events, 0.1 us)
Async XLA Ops:
  3.5 2.3 copy-start.6
  5.5 1.3 copy-start.14
  5.5 1.6 copy-start.13
  5.5 1.6 copy-start.15
  5.6 2.3 copy-start.7
  5.6 3.5 %copy-start.8 = (f32[768]{0:T(1024)S(1)}, f32[768]{0:T(1024)}, u32[]{:S(2)}) copy-start(f32[768]{0:T(1024)} %param.23) | copy-start | bytes 9220
  9.7 104.4 %copy-start.9 = (f32[768]{0:T(1024)S(1)}, f32[768]{0:T(1024)}, u32[]{:S(2)}) copy-start(f32[768]{0:T(1024)} %param.30) | copy-start | bytes 9220
  9.7 104.4 %copy-start.10 = (f32[768]{0:T(1024)S(1)}, f32[768]{0:T(1024)}, u32[]{:S(2)}) copy-start(f32[768]{0:T(1024)} %param.31) | copy-start | bytes 9220
  9.7 104.4 %copy-start.11 = (f32[768]{0:T(1024)S(1)}, f32[768]{0:T(1024)}, u32[]{:S(2)}) copy-start(f32[768]{0:T(1024)} %param.32) | copy-start | bytes 9220
  9.7 104.5 %copy-start.12 = (f32[768]{0:T(1024)S(1)}, f32[768]{0:T(1024)}, u32[]{:S(2)}) copy-start(f32[768]{0:T(1024)} %param.36) | copy-start | bytes 9220
  268.9 1.7 copy-start.3
  270.8 2.0 copy-start.2
  272.8 1.6 copy-start.4
  272.8 2.5 copy-start.5
  274.3 6.4 %copy-start.1 = (f32[512,768]{1,0:T(8,128)S(1)}, f32[512,768]{1,0:T(8,128)}, u32[]{:S(2)}) copy-start(f32[512,768]{1,0:T(8,128)} %get-tuple-element.121) | copy-start | bytes 4718596
  280.7 2.0 copy-start

commit v2 on v1

--- a/solution.py
+++ b/solution.py
@@ -59,6 +59,10 @@
 
 def rows_of(start, size, unit):
     return pl.ds(pl.multiple_of(start, unit), size)
+
+
+def flat(ref):
+    return jnp.reshape(ref[...], (1, ref.shape[0]))
 
 
 class Place:
@@ -257,7 +261,7 @@
         else:
             kept, base, into, size = self.r_far, self.near_bit * part, self.r_near, part
         unit = part & -part
-        step = min(part, 32)
+        step = min(unit, 32)
         self.copy(stage, k).wait_recv()
 
         def add(i, carry):
@@ -345,8 +349,12 @@
     hidden_ref,
     gain_ref,
     shift_ref,
-    wt_ref,
-    bias_ref,
+    wq_ref,
+    wk_ref,
+    wv_ref,
+    bq_ref,
+    bv_ref,
+    bu_ref,
     first_ref,
     wo_ref,
     wu_ref,
@@ -386,7 +394,30 @@
     piece = first_ref.shape[0]
     half = total // 2
     hd = HEAD_DIM
-    pack_rows = wt_ref.shape[0]
+    pack_rows = wt_all.shape[1]
+    v_row = 2 * hd * heads_here
+    turned = jnp.logical_or(m == 1, m == 2)
+
+    def slot_row(slot):
+        return rows_of(hd * jnp.where(turned, (slot + 1) % heads_here, slot), hd, hd)
+
+    bq, bv, bu = flat(bq_ref), flat(bv_ref), flat(bu_ref)
+    bias_parts = []
+    for slot in range(heads_here):
+        row = 2 * hd * slot
+        wt_all[m, row : row + hd, :] = wq_ref[slot_row(slot), :]
+        wt_all[m, row + hd : row + 2 * hd, :] = wk_ref[slot_row(slot), :]
+        here, after = hd * slot, hd * ((slot + 1) % heads_here)
+        own_bias = jnp.where(turned, bq[:, after : after + hd], bq[:, here : here + hd])
+        bias_parts += [own_bias, jnp.zeros_like(own_bias)]
+    wt_all[m, v_row : v_row + piece, :] = wv_ref[...]
+    spare = pack_rows - v_row - piece
+    wt_all[m, v_row + piece :, :] = jnp.zeros((spare, wv_ref.shape[1]), BF)
+    bias_parts += [bv, jnp.zeros((1, spare), F32), bu]
+    bias_row = jnp.concatenate(bias_parts, 1)
+    bias_all[m] = jnp.broadcast_to(bias_row, (8, bias_row.shape[1]))
+    wt_ref = wt_all.at[m]
+    bias_ref = bias_all.at[m]
     place.barrier()
     half_pack = pack_rows // 2
     small = [
@@ -431,9 +462,7 @@
         def _(row=row, rows=rows, row_there=row_there):
             v_ref[row_there : row_there + rows, :] = first_ref[row : row + rows, :]
 
-    normed_ref[...] = layer_norm(hidden_ref[...], gain_ref[...], shift_ref[...]).astype(BF)
-    wt_all[m] = wt_ref[...]
-    bias_all[m] = bias_ref[...]
+    normed_ref[...] = layer_norm(hidden_ref[...], flat(gain_ref), flat(shift_ref)).astype(BF)
 
     for item in small:
         item.start(1)
@@ -477,7 +506,6 @@
         for to, heads in enumerate(HEADS_AT)
         for slot, head in enumerate(heads)
     }
-    v_row = 2 * hd * heads_here
 
     for shard in range(ring):
         out = dot(wt_all[shard], normed_ref[...], 1, 1)
@@ -636,12 +664,15 @@
             moved_copy(i).wait_send()
 
 
-def forward_call(ring, heads_here, length, hidden, gain, shift, wt, bias, first_t, wo, wu, wd):
+def forward_call(
+    ring, heads_here, length, hidden, gain, shift, wq, wk, wv, bq, bv, bu, first_t, wo, wu, wd
+):
     count, width = hidden.shape
     total = ring * count
     hd = HEAD_DIM
     piece = first_t.shape[0]
     others = ring - 1
+    pack_rows = 2 * hd * (heads_here + 1)
     sds = jax.ShapeDtypeStruct
     dma = pltpu.SemaphoreType.DMA
     return pl.pallas_call(
@@ -653,13 +684,13 @@
             sds((heads_here * hd, total), BF),
             sds((heads_here, 1, total), F32),
             sds((heads_here * hd, total), F32),
-            sds((ring,) + wt.shape, BF),
-            sds((ring,) + bias.shape, F32),
+            sds((ring, pack_rows, width), BF),
+            sds((ring, 8, pack_rows + bu.shape[0]), F32),
             sds((ring,) + wo.shape, BF),
             sds((ring,) + wu.shape, BF),
             sds((ring,) + wd.shape, BF),
         ),
-        in_specs=[SM] + [VM] * 6 + [ANY] * 3,
+        in_specs=[SM] + [VM] * 10 + [ANY] * 3,
         out_specs=[VM] * 8 + [ANY] * 3,
         scratch_shapes=[
             pltpu.VMEM((ring, heads_here, 2 * hd, count), BF),
@@ -683,7 +714,7 @@
             collective_id=0, has_side_effects=True, vmem_limit_bytes=VMEM_LIMIT
         ),
         name="forward",
-    )(length, hidden, gain, shift, wt, bias, first_t, wo, wu, wd)
+    )(length, hidden, gain, shift, wq, wk, wv, bq, bv, bu, first_t, wo, wu, wd)
 
 
 def backward_kernel(
@@ -695,7 +726,10 @@
     hidden_ref,
     grad_out_ref,
     pre_gain_ref,
-    rows_ref,
+    b_out_ref,
+    mid_gain_ref,
+    mid_shift_ref,
+    b_down_ref,
     bias_ref,
     qk_hbm,
     v_hbm,
@@ -712,7 +746,9 @@
     layer_ref,
     grad_in_ref,
     first_ref,
-    pack_sum,
+    wq_sum,
+    wk_sum,
+    wv_sum,
     wo_sum,
     wu_sum,
     wd_sum,
@@ -729,10 +765,11 @@
     mid_ref,
     mid_t,
     down_ref,
-    down_t,
+    attn_ref,
     act_ref,
     gup_ref,
     g_ref,
+    pack_held,
     wo_share,
     g_all,
     keys,
@@ -792,10 +829,8 @@
     load("wt", wt_hbm, wt_all)
     place.barrier()
 
-    def row(i):
-        return rows_ref[i : i + 1, :]
-
-    b_out, mid_gain, mid_shift, b_down = row(0), row(1), row(2), row(3)
+    b_out, mid_gain, mid_shift = flat(b_out_ref), flat(mid_gain_ref), flat(mid_shift_ref)
+    b_down, pre_gain = flat(b_down_ref), flat(pre_gain_ref)
     act_ref[0] = jnp.transpose(context_ref[...])
     vector_held[0] = jnp.zeros_like(vector_held[0])
     wo_share[:, out_rows:, :] = jnp.zeros_like(wo_share[:, out_rows:, :])
@@ -820,21 +855,29 @@
     zero_row = jnp.zeros((1, width), F32)
     grad_b_down = lax.fori_loop(0, count // tile, project, zero_row)
     mid_t[...] = jnp.transpose(mid_ref[...])
-    down_t[...] = jnp.transpose(down_ref[...])
-
-    down = Reduce(place, wd_all, bufs[0:5], wd_sum, rsend, rrecv, 0, False)
-    up = Reduce(place, wu_all, bufs[5:10], wu_sum, rsend, rrecv, 1, True)
-    out = Reduce(place, wo_share, bufs[10:15], wo_sum, rsend, rrecv, 2, True)
+
+    half_width = width // 2
+
+    def half_of(share, total_ref, at, part, x_first):
+        window = pl.ds(part * half_width, half_width)
+        here = bufs[5 * at : 5 * at + 5]
+        return Reduce(
+            place, share, here, total_ref.at[window], rsend, rrecv, at, x_first, part * half_width
+        )
+
+    early = (half_of(wd_all, wd_sum, 0, 0, False), half_of(wu_all, wu_sum, 1, 0, True))
+    late = (half_of(wd_all, wd_sum, 2, 1, False), half_of(wu_all, wu_sum, 3, 1, True))
+    out = Reduce(place, wo_share, bufs[20:25], wo_sum, rsend, rrecv, 4, True)
     group = 2 * hd
     packs = [
         Reduce(
             place,
             wu_all,
-            bufs[15 + 5 * i : 20 + 5 * i],
-            pack_sum.at[pl.ds(group * i, group)],
+            bufs[25 + 5 * i : 30 + 5 * i],
+            pack_held.at[pl.ds(group * i, group)],
             rsend,
             rrecv,
-            3 + i,
+            5 + i,
             i % 2 == 0,
             group * i,
         )
@@ -888,7 +931,7 @@
         )
         middle_ref[here, :] = grad_middle
         grad_attn = grad_middle.astype(BF)
-        down_ref[here, :] = grad_attn
+        attn_ref[here, :] = grad_attn
         sums = (
             jnp.sum(grad_attn.astype(F32), 0, keepdims=True),
             jnp.sum(grad * unit, 0, keepdims=True),
@@ -901,7 +944,7 @@
         vector_held[0, ring + 2 + i : ring + 3 + i, 0:width] = value
     for i in range(ring):
         here = slice(i * out_rows, (i + 1) * out_rows)
-        g_ref[here, :] = dot(wo_all[here, :], down_ref[...], 1, 1).astype(BF)
+        g_ref[here, :] = dot(wo_all[here, :], attn_ref[...], 1, 1).astype(BF)
 
     def g_copy(slot, to):
         return remote(
@@ -927,7 +970,7 @@
     for j in range(ring):
         here = rows_of(shard_of(j) * out_rows, out_rows, 16)
         wo_share[shard_of(j), 0:out_rows, :] = dot(
-            context_ref[here, :], down_ref[...], 1, 0
+            context_ref[here, :], attn_ref[...], 1, 0
         ).astype(BF)
         out.copy(0, shard_of(j)).start()
 
@@ -937,24 +980,32 @@
         def weigh(i, carry):
             here = lanes(i * 256, 256)
             wu_all[s, :, here] = dot(mid_t[...], gup_ref[s, :, here], 1, 0).astype(BF)
-            wd_all[s, :, here] = dot(down_t[...], act_ref[s, :, here], 1, 0).astype(BF)
+            rows = rows_of(i * 256, 256, 256)
+            wd_all[s, rows, :] = dot(act_ref[s, :, here], down_ref[...], 0, 0).astype(BF)
             return carry
 
         lax.fori_loop(0, wu_all.shape[2] // 256, weigh, 0)
-        down.copy(0, s).start()
-        up.copy(0, s).start()
+        for item in early + late:
+            item.copy(0, s).start()
 
         @pl.when(j > 0)
         def _():
-            down.fold_one(0, shard_of(j - 1))
-            up.fold_one(0, shard_of(j - 1))
+            for item in early:
+                item.fold_one(0, shard_of(j - 1))
 
         return carry
 
     lax.fori_loop(0, ring, weigh_shard, 0)
+    for item in early:
+        item.fold_one(0, shard_of(ring - 1))
+
+    def fold_late(j, carry):
+        for item in late:
+            item.fold_one(0, shard_of(j))
+        return carry
+
+    lax.fori_loop(0, ring, fold_late, 0)
     out.fold(0)
-    down.fold_one(0, shard_of(ring - 1))
-    up.fold_one(0, shard_of(ring - 1))
     for name in ("v", "qk", "lse", "exact"):
         loads[name].wait()
 
@@ -1022,7 +1073,8 @@
             for name in ("normed", "wt"):
                 loads[name].wait()
             for k in range(ring):
-                up.copy(0, k).wait_send()
+                early[1].copy(0, k).wait_send()
+                late[1].copy(0, k).wait_send()
         if i < heads_here:
             for j in range(1, ring):
                 qk_copy(i, j).wait_recv()
@@ -1105,21 +1157,25 @@
         @pl.when(h == 1)
         def _():
             send_fresh(1)
+            for item in early:
+                item.fold(1)
 
         return carry
 
     lax.fori_loop(0, heads_here, attend_back, 0)
     send_fresh(2)
     send_reused()
-    ffn = (down, up, out)
-    for item in ffn:
+    late = late + (out,)
+    for item in late:
         item.fold(1)
     process(0)
     process(1)
+    for item in early:
+        item.fold(2)
     packs[0].fold(0)
     packs[1].fold(0)
     packs[0].fold(1)
-    for item in ffn:
+    for item in late:
         item.fold(2)
     packs[1].fold(1)
     packs[0].fold(2)
@@ -1168,7 +1224,7 @@
         center = value - jnp.mean(value, -1, keepdims=True)
         scale = lax.rsqrt(jnp.mean(center * center, -1, keepdims=True) + EPSILON)
         unit = center * scale
-        grad_unit = grad * pre_gain_ref[...]
+        grad_unit = grad * pre_gain
         grad_in_ref[here, :] = middle_ref[here, :] + scale * (
             grad_unit
             - jnp.mean(grad_unit, -1, keepdims=True)
@@ -1183,6 +1239,18 @@
     sums = lax.fori_loop(0, count // tile, input_back, (zero_row,) * 2)
     for i, value in enumerate(sums):
         vector_held[0, ring + i : ring + 1 + i, 0:width] = value
+
+    turned = jnp.logical_or(m == 1, m == 2)
+
+    def natural(own_row):
+        parts = []
+        for i in range(heads_here):
+            here, turn = group * i, group * ((i - 1) % heads_here)
+            parts.append(
+                jnp.where(turned, own_row[:, turn : turn + hd], own_row[:, here : here + hd])
+            )
+        parts.append(jnp.zeros((1, own_row.shape[1] - hd * heads_here), F32))
+        return jnp.concatenate(parts, 1)
 
     routes = [place.to_core, place.to_x, place.to_y]
     routes += [place.to_plane(step) for step in place.steps()]
@@ -1203,31 +1271,38 @@
             vector_held[k + 1] = value
             vector_copy(k + 1).start()
         else:
-            vector_sum[...] = value
+            own_row = value[0:1]
+            for s in range(1, ring):
+                own_row = jnp.where(m == s, value[s : s + 1], own_row)
+            vector_sum[...] = jnp.concatenate([value[ring : ring + 6], own_row, natural(own_row)], 0)
 
     vector_copy(0).start()
     first, second, third, fourth = packs
+    for item in early:
+        item.fold_pair()
     second.fold(2)
     third.fold(0)
     fourth.fold(0)
     vector_fold(0)
-    for item in ffn:
+    for item in late:
         item.fold_pair()
     third.fold(1)
     fourth.fold(1)
     vector_fold(1)
     first.fold_pair()
     second.fold_pair()
-    for item in ffn:
+    for item in early:
         item.finish_sum()
     third.fold(2)
     fourth.fold(2)
     vector_fold(2)
     first.finish_sum()
     second.finish_sum()
+    for item in late:
+        item.finish_sum()
     third.fold_pair()
     fourth.fold_pair()
-    for item in ffn:
+    for item in early:
         item.spread(6)
     for k in range(3, len(routes) - 1):
         vector_fold(k)
@@ -1235,26 +1310,35 @@
     second.spread(6)
     third.finish_sum()
     fourth.finish_sum()
-    for item in ffn:
+    for item in late:
+        item.spread(6)
+    for item in early:
         item.spread(7)
     vector_fold(len(routes) - 1)
-    for item in packs:
-        item.spread(6 if item in (third, fourth) else 7)
-    third.spread(7)
-    fourth.spread(7)
-    everything = ffn + tuple(packs)
+    third.spread(6)
+    fourth.spread(6)
+    for item in late + (first, second, third, fourth):
+        item.spread(7)
+    everything = early + late + tuple(packs)
     for item in everything:
         item.wait(7)
-        item.drain(1 if item is up else 0)
+        item.drain(1 if item in (early[1], late[1]) else 0)
     for k in range(len(routes)):
         vector_copy(k).wait_send()
     for h in range(heads_here):
         for j in range(1, ring):
             qk_copy(h, j).wait_send()
+    for i in range(heads_here):
+        at = rows_of(group * jnp.where(turned, (i - 1) % heads_here, i), hd, hd)
+        wq_sum[hd * i : hd * i + hd, :] = pack_held[at, :]
+        at = rows_of(group * jnp.where(turned, (i - 1) % heads_here, i) + hd, hd, hd)
+        wk_sum[hd * i : hd * i + hd, :] = pack_held[at, :]
+    wv_sum[...] = pack_held[v_row : v_row + piece, :]
 
 
 def backward_call(
-    ring, heads_here, planes, length, context, hidden, grad_out, pre_gain, rows, bias,
+    ring, heads_here, planes, length, context, hidden, grad_out, pre_gain, b_out, mid_gain, mid_shift,
+    b_down, bias,
     qk, v, lse, exact, normed, wt, wo, wo_far, wu, wu_far, wd, wd_far, piece,
 ):
     count, width = hidden.shape
@@ -1267,7 +1351,7 @@
     stages = 8 + planes.bit_length() - 1
     pack_rows = wt.shape[1]
     out_pad = wo.shape[0] + -wo.shape[0] % (16 * PLANE)
-    sizes = [wd.shape[0], wu.shape[0], out_pad] + [2 * hd] * (heads_here + 1)
+    sizes = [wd.shape[0] // 2, wu.shape[0] // 2] * 2 + [out_pad] + [2 * hd] * (heads_here + 1)
     bufs = [buf for rows_ in sizes for buf in Reduce.buffers(rows_, width, planes)]
     vector = (ring + 6 + -(ring + 6) % 8, bias.shape[2])
     vm = pltpu.VMEM
@@ -1277,14 +1361,16 @@
             sds(hidden.shape, F32),
             sds(hidden.shape, F32),
             sds((piece, total), BF),
-            sds(wt.shape[1:], BF),
+            sds((heads_here * hd, width), BF),
+            sds((heads_here * hd, width), BF),
+            sds((piece, width), BF),
             sds((out_pad, width), BF),
             sds(wu.shape, BF),
             sds(wd.shape, BF),
-            sds(vector, F32),
+            sds((8, vector[1]), F32),
         ),
-        in_specs=[SM] + [VM] * 6 + [ANY] * 12,
-        out_specs=[VM] * 8,
+        in_specs=[SM] + [VM] * 9 + [ANY] * 12,
+        out_specs=[VM] * 10,
         scratch_shapes=[
             vm(qk.shape, BF),
             vm(v.shape, BF),
@@ -1298,10 +1384,11 @@
             vm((count, width), BF),
             vm((width, count), BF),
             vm((count, width), BF),
-            vm((width, count), BF),
+            vm((count, width), BF),
             vm((ring, count, width), BF),
             vm((ring, count, width), BF),
             vm((width, count), BF),
+            vm((pack_rows, width), BF),
             vm((ring, out_pad, width), BF),
             vm((heads_here, hd, total), BF),
             vm((total, hd), BF),
@@ -1320,8 +1407,8 @@
             dma((len(FRESH), others)),
             dma((1,)),
             dma((1,)),
-            dma((3 + heads_here + 1, stages, ring)),
-            dma((3 + heads_here + 1, stages, ring)),
+            dma((5 + heads_here + 1, stages, ring)),
+            dma((5 + heads_here + 1, stages, ring)),
             dma((hops,)),
             dma((hops,)),
         ]
@@ -1331,7 +1418,7 @@
         ),
         name="backward",
     )(
-        length, context, hidden, grad_out, pre_gain, rows, bias, qk, v, lse, exact,
+        length, context, hidden, grad_out, pre_gain, b_out, mid_gain, mid_shift, b_down, bias, qk, v, lse, exact,
         normed, wt, wo, wo_far, wu, wu_far, wd, wd_far,
     )
 
@@ -1364,52 +1451,25 @@
     head_width = w_query.shape[1]
     heads_here = head_width // hd
     piece = w_value.shape[1]
-    pack_rows = 2 * hd * (heads_here + 1)
-    turned = jnp.logical_or(m == 1, m == 2)
-
-    def to_slots(value):
-        return jnp.where(turned, jnp.roll(value, -1, 0), value)
-
-    def from_slots(value):
-        return jnp.where(turned, jnp.roll(value, 1, 0), value)
-
-    wq = to_slots(w_query.T.reshape(heads_here, 1, hd, width))
-    wk = to_slots(w_key.T.reshape(heads_here, 1, hd, width))
-    spare = pack_rows - 2 * head_width - piece
-    wt = jnp.concatenate(
-        [
-            jnp.concatenate([wq, wk], 1).reshape(2 * head_width, width),
-            w_value.T,
-            jnp.zeros((spare, width), BF),
-        ],
-        0,
-    )
-    bq = to_slots(b_query.reshape(heads_here, 1, hd))
-    bias = jnp.concatenate(
-        [
-            jnp.concatenate([bq, jnp.zeros_like(bq)], 1).reshape(-1),
-            b_value,
-            jnp.zeros((spare,), F32),
-            b_up,
-        ]
-    )
-    bias = jnp.broadcast_to(bias[None], (8, bias.shape[0]))
     context_t, normed, qk, v, lse, exact, wt_all, bias_all, wo_far, wu_far, wd_far = forward_call(
         ring,
         heads_here,
         first_length,
         hidden_in,
-        pre_gain[None],
-        pre_shift[None],
-        wt,
-        bias,
+        pre_gain,
+        pre_shift,
+        w_query.T,
+        w_key.T,
+        w_value.T,
+        b_query,
+        b_value,
+        b_up,
         first_values.T,
         w_out,
         w_up,
         w_down,
     )
-    rows = jnp.stack([b_out, mid_gain, mid_shift, b_down] * 2)
-    layer_out, grad_input, grad_first, pack_sum, wo_sum, wu_sum, wd_sum, vector = backward_call(
+    layer_out, grad_input, grad_first, wq_sum, wk_sum, wv_sum, wo_sum, wu_sum, wd_sum, vector = backward_call(
         ring,
         heads_here,
         lax.axis_size("dp") // PLANE,
@@ -1417,8 +1477,11 @@
         context_t,
         hidden_in,
         grad_out,
-        pre_gain[None],
-        rows,
+        pre_gain,
+        b_out,
+        mid_gain,
+        mid_shift,
+        b_down,
         bias_all,
         qk,
         v,
@@ -1434,28 +1497,26 @@
         wd_far,
         piece,
     )
-    own_vector = lax.dynamic_index_in_dim(vector, m, 0, False)
-    qk_grad = from_slots(pack_sum[: 2 * head_width].astype(F32).reshape(heads_here, 2, hd, width))
-    v_grad = pack_sum[2 * head_width : 2 * head_width + piece].astype(F32)
-    rows = [vector[ring + i, :width] for i in range(6)]
+    pack_rows = wt_all.shape[1]
+    rows = [vector[i, :width] for i in range(6)]
     return (
         layer_out,
         grad_input,
         grad_first.astype(F32).T,
         rows[0],
         rows[1],
-        qk_grad[:, 0].reshape(head_width, width).T,
-        from_slots(own_vector[: 2 * head_width].reshape(heads_here, 2, hd))[:, 0].reshape(-1),
-        qk_grad[:, 1].reshape(head_width, width).T,
-        v_grad.T,
-        own_vector[2 * head_width : 2 * head_width + piece],
+        wq_sum.astype(F32).T,
+        vector[7, :head_width],
+        wk_sum.astype(F32).T,
+        wv_sum.astype(F32).T,
+        vector[6, 2 * head_width : 2 * head_width + piece],
         wo_sum[:head_width].astype(F32),
         rows[2],
         rows[3],
         rows[4],
         wu_sum.astype(F32),
-        own_vector[pack_rows:],
-        wd_sum.astype(F32).T,
+        vector[6, pack_rows:],
+        wd_sum.astype(F32),
         rows[5],
     )
 

time: 285 us -> 266 us (0.933)
  local copies, waits for them, and re-layouts: 19.6 us -> 7.98 us
  Pallas kernels: 254 us -> 247 us
    pallas_call x1, Pallas kernels: 150 us -> 143 us  [backward_call(): pl.pallas_call(functools.partial(backward_kernel, ring, heads_here, plane...]
    slice x13 -> x2, local copies, waits for them, and re-layouts: 8.43 us -> 2.95 us  [the longest x1 1.69 us: shards(): rows = [vector[i, :width] for i in range(6)]]
    unnamed x36 -> x16, local copies, waits for them, and re-layouts: 5.74 us -> 3.77 us
where the time goes in v2:
time: 266 us; the launch traced here: 265 us
  Pallas kernels  247 us (93%)
  other arithmetic  8.64 us (3%)
  local copies, waits for them, and re-layouts  7.98 us (3%)
    pallas_call x1, Pallas kernels, backward_call(): pl.pallas_call(functools.partial(backward_kernel, ring, heads_here, plane...  143 us
    pallas_call x1, Pallas kernels, forward_call(): pl.pallas_call(functools.partial(forward_kernel, ring, heads_here), out_s...  105 us

profile of v2, /device:TPU:0, one launch (start us, length us, event | category | flops | bytes accessed | tf_op | source)
XLA Modules:
  0.0 265.3 jit_solution(17936380173361857872)
XLA Ops:
  1.3 104.8 %forward.1 = (bf16[768,512]{1,0:T(8,128)(2,1)}, bf16[512,768]{1,0:T(8,128)(2,1)}, bf16[3,128,2048]{2,1,0:T(8,128)(2,1)}, bf16[192,2048]{1,0:T(8,128)(2,1)}, f32[...) custom-call(s32[1]{0:T(128)S(6)} %copy.39.length_ref, ...), custom_call_target="tpu_custom_call" | custom-call | tf_op jit(solution)/shard_map/forward/pallas_call | solution.py:678
  106.1 142.6 %backward.1 = (f32[512,768]{1,0:T(8,128)}, f32[512,768]{1,0:T(8,128)}, bf16[96,2048]{1,0:T(8,128)(2,1)}, bf16[192,768]{1,0:T(8,128)(2,1)}, bf16[192,768]{1,0:T(8...) custom-call(s32[1]{0:T(128)S(6)} %copy.39.length_ref, ...), custom_call_target="tpu_custom_call" | custom-call | tf_op jit(solution)/shard_map/backward/pallas_call | solution.py:1358
  248.7 0.0 copy-start.4
  248.7 0.0 copy-start.5
  248.7 0.0 copy-start.6
  248.7 1.3 slice_bitcast_fusion
  249.9 1.3 slice.32
  251.2 1.7 slice_reduce_fusion
  252.9 1.6 convert_bitcast_fusion.3
  254.5 1.8 slice_convert_fusion
  256.4 0.0 copy-done.4
  256.4 0.0 copy-start.3
  256.4 0.9 convert_bitcast_fusion
  257.3 0.0 copy-done.5
  257.3 0.0 copy-done.6
  257.3 1.1 convert_bitcast_fusion.1
  258.4 0.0 copy-done.3
  258.4 0.0 copy-start.2
  258.4 1.6 convert_element_type.14
  260.0 0.1 copy-done.2
  260.1 0.0 copy-start.1
  260.1 1.6 convert_element_type.15
  261.7 0.5 copy-done.1
  262.2 0.0 copy-start
  262.2 1.1 copy.40
  263.3 0.8 copy-done
  264.2 1.1 copy.41
Async XLA Ops:
  248.7 7.7 %copy-start.4 = (bf16[96,2048]{1,0:T(8,128)(2,1)S(1)}, bf16[96,2048]{1,0:T(8,128)(2,1)}, u32[]{:S(2)}) copy-start(bf16[96,2048]{1,0:T(8,128)(2,1)} %get-tuple-element.52) | copy-start | bytes 1179652
  248.7 8.6 %copy-start.5 = (bf16[192,768]{1,0:T(8,128)(2,1)S(1)}, bf16[192,768]{1,0:T(8,128)(2,1)}, u32[]{:S(2)}) copy-start(bf16[192,768]{1,0:T(8,128)(2,1)} %get-tuple-element.54) | copy-start | bytes 884740
  248.7 8.6 %copy-start.6 = (bf16[192,768]{1,0:T(8,128)(2,1)S(1)}, bf16[192,768]{1,0:T(8,128)(2,1)}, u32[]{:S(2)}) copy-start(bf16[192,768]{1,0:T(8,128)(2,1)} %get-tuple-element.55) | copy-start | bytes 884740
  256.4 2.0 copy-start.3
  258.4 1.7 copy-start.2
  260.1 2.1 copy-start.1
  262.2 2.0 copy-start

commit v3 on v2

--- a/solution.py
+++ b/solution.py
@@ -176,10 +176,14 @@
         elif stage == 1:
             self.copy(0, 0).wait_recv()
             self.copy(1, 1).start()
+            self.copy(2, 0).start()
+        elif stage == 2:
+            for k in range(2):
+                self.copy(1, k).wait_recv()
+                self.copy(2, k + 1).start()
         else:
-            for k in range(2 if stage == 2 else 3):
+            for k in range(3):
                 self.copy(stage - 1, k).wait_recv()
-            for k in range(3):
                 self.copy(stage, k).start()
 
     def arrive(self):
@@ -360,16 +364,22 @@
     wu_ref,
     wd_ref,
     context_ref,
-    normed_ref,
-    qk_ref,
-    v_ref,
+    normed_out,
+    qk_out,
+    v_out,
     lse_ref,
-    exact_ref,
-    wt_all,
+    exact_out,
+    wt_out,
     bias_all,
     wo_far,
     wu_far,
     wd_far,
+    normed_ref,
+    qk_ref,
+    v_ref,
+    exact_ref,
+    wt_all,
+    osem,
     y_send,
     vy_send,
     c_send,
@@ -388,6 +398,10 @@
     crecv,
 ):
     place = Place(ring)
+
+    def keep(i, src, dst):
+        return pltpu.make_async_copy(src, dst, osem.at[i])
+
     m = place.m
     count = hidden_ref.shape[0]
     total = ring * count
@@ -574,16 +588,19 @@
         def _(i=i):
             moved_copy(i).wait_recv()
 
+    keep(0, normed_ref, normed_out).start()
+    keep(1, wt_all, wt_out).start()
+    keep(2, v_ref, v_out).start()
     boundary = length_ref[0]
     block = count
 
-    def context_copy(h, j):
+    def context_copy(h, to):
         return remote(
-            c_send.at[rows_of(hd * h, hd, hd), lanes(place.z(j) * count, count)],
+            c_send.at[rows_of(hd * h, hd, hd), pl.ds(to * count, count)],
             context_ref.at[rows_of(place.head(h) * hd, hd, hd)],
-            csend.at[h, j - 1],
-            crecv.at[h, j - 1],
-            place.to_z(j),
+            csend.at[h, to],
+            crecv.at[h, place.shift_to(to) - 1],
+            (place.d, to),
         )
 
     def attend(h, carry):
@@ -621,9 +638,18 @@
             exact_ref[here_h, queries] = result
             c_send[here_h, queries] = result.astype(BF)
             lse_ref[h, :, queries] = top + jnp.log(run_sum)
-        for j in range(1, ring):
-            context_copy(h, j).start()
-        context_ref[rows_of(place.head(h) * hd, hd, hd), :] = c_send[here_h, own]
+
+            @pl.when(m == qi)
+            def _(queries=queries):
+                context_ref[rows_of(place.head(h) * hd, hd, hd), :] = c_send[here_h, queries]
+
+            @pl.when(m != qi)
+            def _(qi=qi):
+                context_copy(h, qi).start()
+
+
+        keep(3 + h, qk_ref.at[h], qk_out.at[h]).start()
+        keep(3 + heads_here + h, exact_ref.at[here_h], exact_out.at[here_h]).start()
 
         @pl.when(h == 1)
         def _():
@@ -637,19 +663,31 @@
         item.arrive()
     for h in range(heads_here):
         for j in range(1, ring):
-            context_copy(h, j).wait_recv()
+            remote(
+                c_send.at[pl.ds(hd * h, hd), own],
+                context_ref.at[pl.ds(0, hd)],
+                csend.at[h, 0],
+                crecv.at[h, j - 1],
+                place.to_z(j),
+            ).wait_recv()
+    keep(0, normed_ref, normed_out).wait()
+    keep(1, wt_all, wt_out).wait()
+    keep(2, v_ref, v_out).wait()
+    for h in range(heads_here):
+        here_h = pl.ds(hd * h, hd)
+        keep(3 + h, qk_ref.at[h], qk_out.at[h]).wait()
+        keep(3 + heads_here + h, exact_ref.at[here_h], exact_out.at[here_h]).wait()
     for item in small + big:
         item.drain()
     for j in range(1, ring):
         bias_copy(j).wait_send()
-        for h in range(heads_here):
-            context_copy(h, j).wait_send()
     for to in range(ring):
 
         @pl.when(m != to)
         def _(to=to):
             for slot in range(heads_here):
                 qk_copy(slot, to).wait_send()
+                context_copy(slot, to).wait_send()
 
     for i, (shard, row, rows, to, row_there) in enumerate(FRESH):
 
@@ -691,8 +729,14 @@
             sds((ring,) + wd.shape, BF),
         ),
         in_specs=[SM] + [VM] * 10 + [ANY] * 3,
-        out_specs=[VM] * 8 + [ANY] * 3,
+        out_specs=[VM] + [ANY] * 3 + [VM] + [ANY] * 2 + [VM] + [ANY] * 3,
         scratch_shapes=[
+            pltpu.VMEM((count, width), BF),
+            pltpu.VMEM((heads_here, 2 * hd, total), BF),
+            pltpu.VMEM((heads_here * hd, total), BF),
+            pltpu.VMEM((heads_here * hd, total), F32),
+            pltpu.VMEM((ring, pack_rows, width), BF),
+            dma((3 + 2 * heads_here,)),
             pltpu.VMEM((ring, heads_here, 2 * hd, count), BF),
             pltpu.VMEM((ring, piece, count), BF),
             pltpu.VMEM((heads_here * hd, total), BF),
@@ -707,7 +751,7 @@
             dma((len(FRESH), others)),
             dma((1,)),
             dma((1,)),
-            dma((heads_here, others)),
+            dma((heads_here, ring)),
             dma((heads_here, others)),
         ],
         compiler_params=pltpu.CompilerParams(
@@ -765,7 +809,7 @@
     mid_ref,
     mid_t,
     down_ref,
-    attn_ref,
+    down_t,
     act_ref,
     gup_ref,
     g_ref,
@@ -775,7 +819,8 @@
     keys,
     vals,
     delta,
-    dq,
+    dk,
+    dv,
     grad_ref,
     vector_held,
     vector_came,
@@ -855,6 +900,7 @@
     zero_row = jnp.zeros((1, width), F32)
     grad_b_down = lax.fori_loop(0, count // tile, project, zero_row)
     mid_t[...] = jnp.transpose(mid_ref[...])
+    down_t[...] = jnp.transpose(down_ref[...])
 
     half_width = width // 2
 
@@ -931,7 +977,7 @@
         )
         middle_ref[here, :] = grad_middle
         grad_attn = grad_middle.astype(BF)
-        attn_ref[here, :] = grad_attn
+        down_ref[here, :] = grad_attn
         sums = (
             jnp.sum(grad_attn.astype(F32), 0, keepdims=True),
             jnp.sum(grad * unit, 0, keepdims=True),
@@ -944,7 +990,7 @@
         vector_held[0, ring + 2 + i : ring + 3 + i, 0:width] = value
     for i in range(ring):
         here = slice(i * out_rows, (i + 1) * out_rows)
-        g_ref[here, :] = dot(wo_all[here, :], attn_ref[...], 1, 1).astype(BF)
+        g_ref[here, :] = dot(wo_all[here, :], down_ref[...], 1, 1).astype(BF)
 
     def g_copy(slot, to):
         return remote(
@@ -970,7 +1016,7 @@
     for j in range(ring):
         here = rows_of(shard_of(j) * out_rows, out_rows, 16)
         wo_share[shard_of(j), 0:out_rows, :] = dot(
-            context_ref[here, :], attn_ref[...], 1, 0
+            context_ref[here, :], down_ref[...], 1, 0
         ).astype(BF)
         out.copy(0, shard_of(j)).start()
 
@@ -980,8 +1026,7 @@
         def weigh(i, carry):
             here = lanes(i * 256, 256)
             wu_all[s, :, here] = dot(mid_t[...], gup_ref[s, :, here], 1, 0).astype(BF)
-            rows = rows_of(i * 256, 256, 256)
-            wd_all[s, rows, :] = dot(act_ref[s, :, here], down_ref[...], 0, 0).astype(BF)
+            wd_all[s, :, here] = dot(down_t[...], act_ref[s, :, here], 1, 0).astype(BF)
             return carry
 
         lax.fori_loop(0, wu_all.shape[2] // 256, weigh, 0)
@@ -1009,13 +1054,13 @@
     for name in ("v", "qk", "lse", "exact"):
         loads[name].wait()
 
-    def qk_copy(h, j):
+    def qk_copy(h, to):
         return remote(
-            qk_ref.at[h, :, lanes(place.z(j) * count, count)],
+            qk_ref.at[h, :, pl.ds(to * count, count)],
             grad_ref.at[place.shard(h), rows_of(2 * hd * h, 2 * hd, 2 * hd)],
-            qsend.at[h, j - 1],
-            qrecv.at[h, j - 1],
-            place.to_z(j),
+            qsend.at[h, to],
+            qrecv.at[h, place.shift_to(to) - 1],
+            (place.d, to),
         )
 
     v_row = 2 * hd * heads_here
@@ -1077,7 +1122,13 @@
                 late[1].copy(0, k).wait_send()
         if i < heads_here:
             for j in range(1, ring):
-                qk_copy(i, j).wait_recv()
+                remote(
+                    qk_ref.at[i, :, own],
+                    grad_ref.at[0, pl.ds(2 * hd * i, 2 * hd)],
+                    qsend.at[i, 0],
+                    qrecv.at[i, j - 1],
+                    place.to_z(j),
+                ).wait_recv()
         begin = group * i
         here = slice(begin, begin + group)
         for k in range(ring):
@@ -1115,18 +1166,17 @@
         delta[...] = jnp.sum(
             g_all[h].astype(F32) * exact_ref[here_h, :], 0, keepdims=True
         )
-        for ki in range(ring):
-            key_start = ki * block
-            key_rows = keys[key_start : key_start + block, :]
-            val_rows = vals[key_start : key_start + block, :]
-            key_t = qk_ref[h, hd : 2 * hd, key_start : key_start + block]
-            grad_k = None
-            for qi in range(ki, ring):
-                query_start = qi * block
-                here = slice(query_start, query_start + block)
-                q = qk_ref[h, 0:hd, here]
-                g = g_all[h, :, here]
-                scores = dot(key_rows, q, 1, 0) - lse_ref[h, :, here]
+        for qi in reversed(range(ring)):
+            query_start = qi * block
+            here = slice(query_start, query_start + block)
+            q = qk_ref[h, 0:hd, here]
+            g = g_all[h, :, here]
+            grad_q = None
+            for ki in range(qi + 1):
+                key_start = ki * block
+                there = slice(key_start, key_start + block)
+                key_t = qk_ref[h, hd : 2 * hd, there]
+                scores = dot(keys[there, :], q, 1, 0) - lse_ref[h, :, here]
                 if ki == qi:
                     scores = jnp.where(
                         diagonal_mask(scores, key_start, query_start), scores, NEG_LARGE
@@ -1134,25 +1184,29 @@
                 elif key_start < half <= query_start:
                     scores = scores + other_document(boundary, key_start, query_start)
                 p = jnp.exp(scores)
-                grad_p = dot(val_rows, g, 1, 0)
+                grad_p = dot(vals[there, :], g, 1, 0)
                 grad_s = (p * (grad_p - delta[:, here])).astype(BF)
-                part_v = dot(g, p.astype(BF), 1, 1)
-                part_k = dot(q, grad_s, 1, 1)
-                if grad_k is None:
-                    grad_v, grad_k = part_v, part_k
-                else:
-                    grad_v, grad_k = grad_v + part_v, grad_k + part_k
+                grad_v = dot(g, p.astype(BF), 1, 1)
+                grad_k = dot(q, grad_s, 1, 1)
                 part_q = dot(key_t, grad_s, 1, 0)
-                if ki == 0:
-                    dq[:, here] = part_q
-                else:
-                    dq[:, here] += part_q
-            qk_ref[h, hd : 2 * hd, key_start : key_start + block] = grad_k.astype(BF)
-            v_ref[here_h, key_start : key_start + block] = grad_v.astype(BF)
-        qk_ref[h, 0:hd, :] = (dq[...] * (hd**-0.5)).astype(BF)
-        for j in range(1, ring):
-            qk_copy(h, j).start()
-        grad_ref[place.shard(h), rows_of(2 * hd * h, 2 * hd, 2 * hd), :] = qk_ref[h, :, own]
+                grad_q = part_q if grad_q is None else grad_q + part_q
+                if qi < ring - 1:
+                    grad_v, grad_k = grad_v + dv[:, there], grad_k + dk[:, there]
+                if ki < qi:
+                    dv[:, there], dk[:, there] = grad_v, grad_k
+            qk_ref[h, 0:hd, here] = (grad_q * (hd**-0.5)).astype(BF)
+            qk_ref[h, hd : 2 * hd, here] = grad_k.astype(BF)
+            v_ref[here_h, here] = grad_v.astype(BF)
+
+            @pl.when(m == qi)
+            def _(here=here):
+                grad_ref[place.shard(h), rows_of(2 * hd * h, 2 * hd, 2 * hd), :] = qk_ref[
+                    h, :, here
+                ]
+
+            @pl.when(m != qi)
+            def _(qi=qi):
+                qk_copy(h, qi).start()
 
         @pl.when(h == 1)
         def _():
@@ -1325,9 +1379,13 @@
         item.drain(1 if item in (early[1], late[1]) else 0)
     for k in range(len(routes)):
         vector_copy(k).wait_send()
-    for h in range(heads_here):
-        for j in range(1, ring):
-            qk_copy(h, j).wait_send()
+    for to in range(ring):
+
+        @pl.when(m != to)
+        def _(to=to):
+            for h in range(heads_here):
+                qk_copy(h, to).wait_send()
+
     for i in range(heads_here):
         at = rows_of(group * jnp.where(turned, (i - 1) % heads_here, i), hd, hd)
         wq_sum[hd * i : hd * i + hd, :] = pack_held[at, :]
@@ -1384,7 +1442,7 @@
             vm((count, width), BF),
             vm((width, count), BF),
             vm((count, width), BF),
-            vm((count, width), BF),
+            vm((width, count), BF),
             vm((ring, count, width), BF),
             vm((ring, count, width), BF),
             vm((width, count), BF),
@@ -1395,13 +1453,14 @@
             vm((total, hd), BF),
             vm((1, total), F32),
             vm((hd, total), F32),
+            vm((hd, total), F32),
             vm((ring, pack_rows, count), BF),
             vm((hops,) + vector, F32),
             vm((hops,) + vector, F32),
             dma((3 * ring + 6,)),
             dma((heads_here, ring)),
             dma((heads_here, others)),
-            dma((heads_here, others)),
+            dma((heads_here, ring)),
             dma((heads_here, others)),
             dma((len(FRESH), others)),
             dma((len(FRESH), others)),
@@ -1421,6 +1480,51 @@
         length, context, hidden, grad_out, pre_gain, b_out, mid_gain, mid_shift, b_down, bias, qk, v, lse, exact,
         normed, wt, wo, wo_far, wu, wu_far, wd, wd_far,
     )
+
+
+def finish_kernel(count_in, turned, pieces, vector_ref, *refs):
+    ins, refs = refs[:count_in], refs[count_in:]
+    outs, refs = refs[:count_in], refs[count_in:]
+    rows, refs = refs[: len(pieces)], refs[len(pieces) :]
+    held, wide, sem_in, sem_out = refs[:count_in], refs[count_in:-2], refs[-2], refs[-1]
+    rising = iter(wide)
+    loads = [pltpu.make_async_copy(a, b, sem_in.at[i]) for i, (a, b) in enumerate(zip(ins, held))]
+    for load in loads:
+        load.start()
+    for ref, (row, start, size) in zip(rows, pieces):
+        ref[...] = jnp.reshape(vector_ref[row : row + 1, start : start + size], (size,))
+    stores = []
+    for i in range(count_in):
+        loads[i].wait()
+        source = held[i]
+        if source.dtype != F32:
+            into = next(rising)
+            value = source[0 : into.shape[0], :]
+            if i == turned:
+                value = jnp.transpose(value)
+            into[...] = value.astype(F32)
+            source = into
+        stores.append(pltpu.make_async_copy(source, outs[i], sem_out.at[i]))
+        stores[i].start()
+    for store in stores:
+        store.wait()
+
+
+def finish_call(vector, pieces, arrays, rows, turned):
+    sds = jax.ShapeDtypeStruct
+    dma = pltpu.SemaphoreType.DMA
+    shapes = [(rows_, array.shape[1]) for array, rows_ in zip(arrays, rows)]
+    return pl.pallas_call(
+        functools.partial(finish_kernel, len(arrays), turned, pieces),
+        out_shape=[sds(shape, F32) for shape in shapes] + [sds((p[2],), F32) for p in pieces],
+        in_specs=[VM] + [ANY] * len(arrays),
+        out_specs=[ANY] * len(arrays) + [VM] * len(pieces),
+        scratch_shapes=[pltpu.VMEM(array.shape, array.dtype) for array in arrays]
+        + [pltpu.VMEM(s, F32) for s, array in zip(shapes, arrays) if array.dtype != F32]
+        + [dma((len(arrays),)), dma((len(arrays),))],
+        compiler_params=pltpu.CompilerParams(vmem_limit_bytes=VMEM_LIMIT),
+        name="finish",
+    )(vector, *arrays)
 
 
 def shards(
@@ -1498,26 +1602,36 @@
         piece,
     )
     pack_rows = wt_all.shape[1]
-    rows = [vector[i, :width] for i in range(6)]
+    pieces = [(i, 0, width) for i in range(6)] + [
+        (7, 0, head_width),
+        (6, 2 * head_width, piece),
+        (6, pack_rows, b_up.shape[0]),
+    ]
+    arrays = [layer_out, grad_input, wu_sum, wd_sum, grad_first, wq_sum, wk_sum, wo_sum, wv_sum]
+    rows = [count, count, width, w_down.shape[0], piece, head_width, head_width, head_width, piece]
+    done = finish_call(vector, pieces, arrays, rows, 3)
+    layer_out, grad_input, wu_sum, wd_sum, grad_first, wq_sum, wk_sum, wo_sum, wv_sum = done[:9]
+    pre_gain_sum, pre_shift_sum, b_out_sum, mid_gain_sum, mid_shift_sum, b_down_sum = done[9:15]
+    b_query_sum, b_value_sum, b_up_sum = done[15:]
     return (
         layer_out,
         grad_input,
-        grad_first.astype(F32).T,
-        rows[0],
-        rows[1],
-        wq_sum.astype(F32).T,
-        vector[7, :head_width],
-        wk_sum.astype(F32).T,
-        wv_sum.astype(F32).T,
-        vector[6, 2 * head_width : 2 * head_width + piece],
-        wo_sum[:head_width].astype(F32),
-        rows[2],
-        rows[3],
-        rows[4],
-        wu_sum.astype(F32),
-        vector[6, pack_rows:],
-        wd_sum.astype(F32),
-        rows[5],
+        grad_first.T,
+        pre_gain_sum,
+        pre_shift_sum,
+        wq_sum.T,
+        b_query_sum,
+        wk_sum.T,
+        wv_sum.T,
+        b_value_sum,
+        wo_sum,
+        b_out_sum,
+        mid_gain_sum,
+        mid_shift_sum,
+        wu_sum,
+        b_up_sum,
+        wd_sum,
+        b_down_sum,
     )
 
 

time: 266 us -> 254 us (0.955)
  other arithmetic: 8.64 us -> 0 us
  local copies, waits for them, and re-layouts: 7.98 us -> 0 us
  Pallas kernels: 247 us -> 253 us
    pallas_call x0 -> x1, Pallas kernels: none -> 7.25 us  [finish_call(): pl.pallas_call(functools.partial(finish_kernel, len(arrays), turned, piec...]
    convert_element_type x3 -> x0, other arithmetic: 4.97 us -> none  [the longest x1 1.81 us: shards(): wo_sum[:head_width].astype(F32)]
    unnamed x16 -> x0, local copies, waits for them, and re-layouts: 3.77 us -> none
    transpose x3 -> x0, other arithmetic: 3.68 us -> none  [the longest x1 1.64 us: shards(): wv_sum.astype(F32)]
    slice x2 -> x0, local copies, waits for them, and re-layouts: 2.95 us -> none  [the longest x1 1.69 us: shards(): rows = [vector[i, :width] for i in range(6)]]
where the time goes in v3:
time: 254 us
  Pallas kernels  253 us (100%)
    pallas_call x1, Pallas kernels, backward_call(): pl.pallas_call(functools.partial(backward_kernel, ring, heads_here, plane...  141 us
    pallas_call x1, Pallas kernels, forward_call(): pl.pallas_call(functools.partial(forward_kernel, ring, heads_here), out_s...  104 us
    pallas_call x1, Pallas kernels, finish_call(): pl.pallas_call(functools.partial(finish_kernel, len(arrays), turned, piec...  7.25 us

profile of v3, /device:TPU:0, one launch (start us, length us, event | category | flops | bytes accessed | tf_op | source)
XLA Modules:
  0.0 254.1 jit_solution(12625031112666024436)
XLA Ops:
  1.3 104.5 %forward.1 = (bf16[768,512]{1,0:T(8,128)(2,1)}, bf16[512,768]{1,0:T(8,128)(2,1)}, bf16[3,128,2048]{2,1,0:T(8,128)(2,1)}, bf16[192,2048]{1,0:T(8,128)(2,1)}, f32[...) custom-call(s32[1]{0:T(128)S(6)} %copy.37.length_ref, ...), custom_call_target="tpu_custom_call" | custom-call | tf_op jit(solution)/shard_map/forward/pallas_call | solution.py:716
  105.8 140.9 %backward.1 = (f32[512,768]{1,0:T(8,128)}, f32[512,768]{1,0:T(8,128)}, bf16[96,2048]{1,0:T(8,128)(2,1)}, bf16[192,768]{1,0:T(8,128)(2,1)}, bf16[192,768]{1,0:T(8...) custom-call(s32[1]{0:T(128)S(6)} %copy.37.length_ref, ...), custom_call_target="tpu_custom_call" | custom-call | tf_op jit(solution)/shard_map/backward/pallas_call | solution.py:1416
  246.7 7.3 %finish.1 = (f32[512,768]{1,0:T(8,128)}, f32[512,768]{1,0:T(8,128)}, f32[768,768]{1,0:T(8,128)}, f32[768,768]{1,0:T(8,128)}, f32[96,2048]{1,0:T(8,128)}, /*index...) custom-call(f32[8,1280]{1,0:T(8,128)} %get-tuple-element.68.vector_r, ...), custom_call_target="tpu_custom_call" | custom-call | tf_op jit(solution)/shard_map/finish/pallas_call | solution.py:1517

commit v4 on v3

--- a/solution.py
+++ b/solution.py
@@ -787,7 +787,7 @@
     wu_far_hbm,
     wd_hbm,
     wd_far_hbm,
-    layer_ref,
+    layer_out_ref,
     grad_in_ref,
     first_ref,
     wq_sum,
@@ -797,6 +797,7 @@
     wu_sum,
     wd_sum,
     vector_sum,
+    layer_ref,
     qk_ref,
     v_ref,
     lse_ref,
@@ -960,6 +961,8 @@
         return carry
 
     lax.fori_loop(0, ring, feed_shard, 0)
+    layer_copy = pltpu.make_async_copy(layer_ref, layer_out_ref, lsem.at[3 * ring + 6])
+    layer_copy.start()
     load("normed", normed_hbm, mid_ref)
 
     def middle_back(i, carry):
@@ -1270,6 +1273,8 @@
 
     process(2)
     process(3)
+    for item in early:
+        item.fold_pair()
 
     def input_back(i, carry):
         here = rows_of(i * tile, tile, tile)
@@ -1332,8 +1337,6 @@
 
     vector_copy(0).start()
     first, second, third, fourth = packs
-    for item in early:
-        item.fold_pair()
     second.fold(2)
     third.fold(0)
     fourth.fold(0)
@@ -1373,6 +1376,7 @@
     fourth.spread(6)
     for item in late + (first, second, third, fourth):
         item.spread(7)
+    layer_copy.wait()
     everything = early + late + tuple(packs)
     for item in everything:
         item.wait(7)
@@ -1428,8 +1432,9 @@
             sds((8, vector[1]), F32),
         ),
         in_specs=[SM] + [VM] * 9 + [ANY] * 12,
-        out_specs=[VM] * 10,
+        out_specs=[ANY] + [VM] * 9,
         scratch_shapes=[
+            vm((count, width), F32),
             vm(qk.shape, BF),
             vm(v.shape, BF),
             vm(lse.shape, F32),
@@ -1457,7 +1462,7 @@
             vm((ring, pack_rows, count), BF),
             vm((hops,) + vector, F32),
             vm((hops,) + vector, F32),
-            dma((3 * ring + 6,)),
+            dma((3 * ring + 7,)),
             dma((heads_here, ring)),
             dma((heads_here, others)),
             dma((heads_here, ring)),

time: 254 us -> 252 us (level)
  Pallas kernels: 253 us -> 250 us
where the time goes in v4:
time: 252 us
  Pallas kernels  250 us (99%)
    pallas_call x1, Pallas kernels, backward_call(): pl.pallas_call(functools.partial(backward_kernel, ring, heads_here, plane...  139 us
    pallas_call x1, Pallas kernels, forward_call(): pl.pallas_call(functools.partial(forward_kernel, ring, heads_here), out_s...  104 us
    pallas_call x1, Pallas kernels, finish_call(): pl.pallas_call(functools.partial(finish_kernel, len(arrays), turned, piec...  7.25 us

profile of v4, /device:TPU:0, one launch (start us, length us, event | category | flops | bytes accessed | tf_op | source)
XLA Modules:
  0.0 252.0 jit_solution(17345479826381495026)
XLA Ops:
  1.3 104.5 %forward.1 = (bf16[768,512]{1,0:T(8,128)(2,1)}, bf16[512,768]{1,0:T(8,128)(2,1)}, bf16[3,128,2048]{2,1,0:T(8,128)(2,1)}, bf16[192,2048]{1,0:T(8,128)(2,1)}, f32[...) custom-call(s32[1]{0:T(128)S(6)} %copy.37.length_ref, ...), custom_call_target="tpu_custom_call" | custom-call | tf_op jit(solution)/shard_map/forward/pallas_call | solution.py:716
  105.8 138.8 %backward.1 = (f32[512,768]{1,0:T(8,128)}, f32[512,768]{1,0:T(8,128)}, bf16[96,2048]{1,0:T(8,128)(2,1)}, bf16[192,768]{1,0:T(8,128)(2,1)}, bf16[192,768]{1,0:T(8...) custom-call(s32[1]{0:T(128)S(6)} %copy.37.length_ref, ...), custom_call_target="tpu_custom_call" | custom-call | tf_op jit(solution)/shard_map/backward/pallas_call | solution.py:1420
  244.5 7.3 %finish.1 = (f32[512,768]{1,0:T(8,128)}, f32[512,768]{1,0:T(8,128)}, f32[768,768]{1,0:T(8,128)}, f32[768,768]{1,0:T(8,128)}, f32[96,2048]{1,0:T(8,128)}, /*index...) custom-call(f32[8,1280]{1,0:T(8,128)} %get-tuple-element.68.vector_r, ...), custom_call_target="tpu_custom_call" | custom-call | tf_op jit(solution)/shard_map/finish/pallas_call | solution.py:1522
